TPU v7x, 128 devices: a whole 4x4x4 slice. The times are simulated.
128 devices in a mesh: gx: 8 (over z_lo, x), gy: 16 (over z_hi, y, core).
Axes of the slice: x: 4, y: 4, z: 4 (z_hi: 2, z_lo: 2; z = z_hi * 2 + z_lo), core: 2. Of those that a mesh axis runs over, the one named last changes fastest.
Arguments:
- gradient: float32 [16, 1024, 2048], P(None, 'gy', 'gx'), may hold values from -6 to 6
- members: float32 [8, 16, 512, 1024], P(None, None, 'gy', 'gx'), may hold values from -6 to 6
Outputs:
- covariance_product: float32 [16, 1024, 2048], P(None, 'gy', 'gx')
All inputs are finite; a program needn't handle non-finite values.
Results may differ from a plain program's by a relative error of at most 0.0001.
Values sent between devices are 32-bit elements; how exact they have to be, the bound alone decides.
A program may use at most 128 MiB of HBM per device.

v0:
```python
import functools

import jax
import jax.numpy as jnp
import ml_dtypes
import numpy as np
from jax import lax
from jax.experimental import pallas as pl
from jax.experimental.pallas import tpu as pltpu
from jax.sharding import PartitionSpec as P

MESH = pl.DeviceIdType.MESH
F32, BF16 = jnp.float32, jnp.bfloat16
LEV, MEM = 16, 8
CHUNKS = 4
MPAD = 40
APAD = 72

beta_raw = [(1.0 - (offset - 4) ** 2 / 25.0) ** 2 for offset in range(9)]
beta_taps = [value / sum(beta_raw) for value in beta_raw]
generations = ((1, 0.5), (2, 0.075), (4, 0.0125))
row_taps = [beta_taps[4 + k] / beta_taps[4] for k in range(5)]


def halves(matrix):
    hi = matrix.astype(ml_dtypes.bfloat16)
    lo = (matrix - hi.astype(np.float64)).astype(ml_dtypes.bfloat16)
    return np.stack([hi, lo])


def band(outputs):
    matrix = np.zeros((outputs + 8, outputs))
    for column in range(outputs):
        matrix[column : column + 9, column] = beta_taps
    return matrix


def column_filter(factor, weight, west_edge, east_edge):
    count = 128 // factor
    inside = np.ones(count + 8)
    if west_edge:
        inside[:4] = 0.0
    if east_edge:
        inside[-4:] = 0.0
    both = band(count + 8) @ (inside[:, None] * band(count))
    both = np.repeat(both, factor, axis=1) * (weight / (MEM - 1) * beta_taps[4] ** 2)
    result = np.zeros((256, 128 * factor))
    for part in range(factor):
        columns = slice(part * 128, part * 128 + 128)
        start = part * count
        result[start : start + count, columns] = both[8 : count + 8]
        result[128 + start : 136 + start, columns] = both[:8]
        result[136 + start : 144 + start, columns] = both[count + 8 :]
    return halves(result)


def constants():
    filters = []
    for factor, weight in generations:
        kinds = [column_filter(factor, weight, *edges) for edges in ((True, False), (False, False), (False, True))]
        filters.append(np.stack(kinds))
    pairs = np.zeros((256, 128))
    reduce_columns = np.zeros((256, 128))
    for lane in range(128):
        pairs[2 * lane : 2 * lane + 2, lane] = 1.0
        reduce_columns[2 * lane, lane] = 1.0
        reduce_columns[2 * lane + 1, lane] = 0.5
        if lane:
            reduce_columns[2 * lane - 1, lane] = 0.5
    small = np.stack([pairs, reduce_columns]).astype(ml_dtypes.bfloat16)
    spread = np.zeros((256, 256))
    for lane in range(128):
        spread[lane, 2 * lane] = 1.0
        spread[lane, 2 * lane + 1] = 0.5
        spread[lane + 1, 2 * lane + 1] = 0.5
    return filters, small, spread.astype(ml_dtypes.bfloat16)


def split(value):
    hi = value.astype(BF16)
    return hi, (value - hi.astype(F32)).astype(BF16)


def dot(a, b):
    return jnp.dot(a, b, preferred_element_type=F32)


def exact_dot(value, matrix):
    rows = value.shape[0]
    hi, lo = split(value)
    both = dot(jnp.concatenate([hi, lo], axis=0), matrix)
    return both[:rows] + both[rows:]


def full_dot(value, hi_matrix, lo_matrix):
    hi, lo = split(value)
    return dot(hi, hi_matrix) + dot(lo, hi_matrix) + dot(hi, lo_matrix)


def roll(value, shift):
    shift %= 128
    return value if shift == 0 else pltpu.roll(value, shift, 1)


def main_kernel(
    nx, ny,
    g_hbm, m_hbm, w1_hbm, w2_hbm, w4_hbm, small_hbm,
    comb, extra,
    gv, mv, w1, w2, w4, small,
    ac, cz, px, p2x, p4x, y1, y2, y4, sp, rp, o2, o4,
    col_out, col_in, row_out, row_in, corner_out, corner_in,
    end_row_in, end_col_out, end_col_in, end_corner_in,
    local_sem, s1, r1, ys, yr, xs, xr, s3, r3,
):
    gx, gy = lax.axis_index("gx"), lax.axis_index("gy")
    has_w, has_e = gx > 0, gx < nx - 1
    has_s, has_n = gy > 0, gy < ny - 1

    kind = 1 - (gx == 0).astype(jnp.int32) + (gx == nx - 1).astype(jnp.int32)
    g_copies = [
        pltpu.make_async_copy(g_hbm.at[:, :, pl.ds(side * 128, 128)], gv.at[side], local_sem.at[side * 6])
        for side in range(2)
    ]
    m_copy = pltpu.make_async_copy(m_hbm, mv.at[:, :, pl.ds(0, 32), :], local_sem.at[1])
    small_copy = pltpu.make_async_copy(small_hbm, small, local_sem.at[2])
    w1_copy = pltpu.make_async_copy(w1_hbm.at[kind], w1, local_sem.at[3])
    w2_copy = pltpu.make_async_copy(w2_hbm.at[kind], w2, local_sem.at[4])
    w4_copy = pltpu.make_async_copy(w4_hbm.at[kind], w4, local_sem.at[5])
    for copy in (*g_copies, small_copy, m_copy, w1_copy, w2_copy, w4_copy):
        copy.start()

    barrier = pltpu.get_barrier_semaphore()
    around = [
        (has_w, -1, 0), (has_e, 1, 0), (has_s, 0, -1), (has_n, 0, 1),
        (has_w & has_s, -1, -1), (has_e & has_n, 1, 1),
    ]

    def at(dx, dy):
        return {"gx": gx + dx, "gy": gy + dy}

    for there, dx, dy in around:
        @pl.when(there)
        def _(dx=dx, dy=dy):
            pl.semaphore_signal(barrier, inc=1, device_id=at(dx, dy), device_id_type=MESH)

    @pl.when(jnp.logical_not(has_s))
    def _():
        px[:, pl.ds(0, 8)] = jnp.zeros((CHUNKS, 8, 32, 128), F32)
        p2x[:, pl.ds(0, 4)] = jnp.zeros((CHUNKS, 4, 16, 128), F32)
        p4x[:, pl.ds(0, 4)] = jnp.zeros((CHUNKS, 4, 8, 128), F32)
        row_in[...] = jnp.zeros((16, 128), F32)

    @pl.when(jnp.logical_not(has_n))
    def _():
        px[:, pl.ds(40, 8)] = jnp.zeros((CHUNKS, 8, 32, 128), F32)
        p2x[:, pl.ds(28, 4)] = jnp.zeros((CHUNKS, 4, 16, 128), F32)
        p4x[:, pl.ds(20, 4)] = jnp.zeros((CHUNKS, 4, 8, 128), F32)
        end_row_in[...] = jnp.zeros((16, 128), F32)

    @pl.when(jnp.logical_not(has_w))
    def _():
        rp[0] = jnp.zeros((CHUNKS, 112, 128), F32)
        col_in[...] = jnp.zeros((8, 128), F32)

    @pl.when(jnp.logical_not(has_e))
    def _():
        rp[1] = jnp.zeros((CHUNKS, 112, 128), F32)
        end_col_in[...] = jnp.zeros((16, 128), F32)

    @pl.when(jnp.logical_not(has_w & has_s))
    def _():
        corner_in[...] = jnp.zeros((16, 128), F32)

    @pl.when(jnp.logical_not(has_e & has_n))
    def _():
        end_corner_in[...] = jnp.zeros((16, 128), F32)

    def remote(src, dst, send, recv, dx, dy):
        return pltpu.make_async_remote_copy(
            src_ref=src, dst_ref=dst, send_sem=send, recv_sem=recv, device_id=at(dx, dy), device_id_type=MESH
        )

    col_copy = remote(col_out, col_in, s1.at[0], r1.at[0], 1, 0)
    row_copy = remote(row_out, row_in, s1.at[1], r1.at[1], 0, 1)
    corner_copy = remote(corner_out, corner_in, s1.at[2], r1.at[2], 1, 1)
    end_row_copy = remote(comb.at[0], end_row_in, s3.at[0], r3.at[0], 0, -1)
    end_col_copy = remote(end_col_out, end_col_in, s3.at[1], r3.at[1], -1, 0)
    end_corner_copy = remote(end_col_out, end_corner_in, s3.at[2], r3.at[2], -1, -1)

    def y_copies(c, direction):
        if direction == 0:
            places = ((px, 32, 0, 8), (p2x, 16, 0, 4), (p4x, 8, 0, 4))
            dy = 1
        else:
            places = ((px, 8, 40, 8), (p2x, 12, 28, 4), (p4x, 12, 20, 4))
            dy = -1
        return [
            remote(ref.at[c, pl.ds(src, n)], ref.at[c, pl.ds(dst, n)], ys.at[direction, c, i], yr.at[direction, c, i], 0, dy)
            for i, (ref, src, dst, n) in enumerate(places)
        ]

    def x_copy(c, direction):
        if direction == 0:
            return remote(sp.at[0, c], rp.at[0, c], xs.at[0, c], xr.at[0, c], 1, 0)
        return remote(sp.at[1, c], rp.at[1, c], xs.at[1, c], xr.at[1, c], -1, 0)

    lane = lax.broadcasted_iota(jnp.int32, (8, 128), 1)
    first_lane = lane == 0

    for copy in g_copies:
        copy.wait()
    gr = gv.at[1].reshape(LEV * 64, 128)
    parts = []
    for quarter in range(4):
        packed = jnp.zeros((8, 128), F32)
        for i in range(quarter * 32, quarter * 32 + 32):
            value = gr[pl.ds(i * 8, 8), :]
            packed = jnp.where(lane == i, roll(value, i + 1), packed)
        parts.append(packed)
    col_out[...] = jnp.where(lane < 64, jnp.where(lane < 32, parts[0], parts[1]), jnp.where(lane < 96, parts[2], parts[3]))
    for h in range(2):
        corner_out[pl.ds(h * 8, 8), :] = gr[pl.ds(h * 8 * 64 + 63, 8, stride=64), :]

    small_copy.wait()

    def reduce_columns(l, carry):
        ac[l, pl.ds(0, 64), :] = exact_dot(jnp.concatenate([gv[0, l], gv[1, l]], axis=1), small[1])
        return carry

    lax.fori_loop(0, LEV, reduce_columns, 0)
    ar = ac.reshape(LEV * APAD, 128)

    def across_row(y, h):
        return ar[pl.ds(h * 8 * APAD + y, 8, stride=APAD), :]

    for h in range(2):
        row_out[pl.ds(h * 8, 8), :] = across_row(63, h)

    pl.semaphore_wait(barrier, sum(there.astype(jnp.int32) for there, _, _ in around))

    @pl.when(has_e)
    def _():
        col_copy.start()

    @pl.when(has_n)
    def _():
        row_copy.start()

    @pl.when(has_e & has_n)
    def _():
        corner_copy.start()

    @pl.when(has_w)
    def _():
        col_copy.wait_recv()
        value = 0.5 * col_in[...]
        for l in range(LEV):
            for block in range(8):
                tile = ac[l, pl.ds(block * 8, 8), :]
                ac[l, pl.ds(block * 8, 8), :] = tile + jnp.where(first_lane, roll(value, -(l * 8 + block)), 0.0)

    @pl.when(has_s)
    def _():
        row_copy.wait_recv()

    @pl.when(has_w & has_s)
    def _():
        corner_copy.wait_recv()

    before = []
    for h in range(2):
        corner = corner_in[pl.ds(h * 8, 8), :]
        before.append(row_in[pl.ds(h * 8, 8), :] + jnp.where(first_lane, 0.5 * roll(corner, 1), 0.0))

    def reduce_rows(j, carry):
        odd_rows = []
        for h in range(2):
            odd = across_row(2 * j + 1, h)
            cz[j, pl.ds(h * 8, 8), :] = across_row(2 * j, h) + 0.5 * (odd + carry[h])
            odd_rows.append(odd)
        return tuple(odd_rows)

    lax.fori_loop(0, 32, reduce_rows, tuple(before))

    mr = mv.reshape(MEM * LEV * MPAD, 128)

    def member(c, m2, h, y):
        return mr[pl.ds(((2 * c + m2) * LEV + h * 8) * MPAD + y, 8, stride=MPAD), :]

    def half_blocks(c, first, count):
        rows = []
        for k in range(count):
            pair = px[c, 2 * (first + k) - 8] + px[c, 2 * (first + k) - 7]
            for m2 in range(2):
                rows.append(jnp.concatenate([pair[m2 * 16 : m2 * 16 + 8], pair[m2 * 16 + 8 : m2 * 16 + 16]], axis=1))
        value = exact_dot(jnp.concatenate(rows, axis=0), small[0])
        p2x[c, pl.ds(first, count)] = value.reshape(count, 16, 128)

    def quarter_blocks(c, first, count):
        rows = []
        for k in range(count):
            pair = p2x[c, 2 * (first + k) - 8] + p2x[c, 2 * (first + k) - 7]
            rows.append(jnp.concatenate([pair[:8], pair[8:]], axis=1))
        value = exact_dot(jnp.concatenate(rows, axis=0), small[0])
        p4x[c, pl.ds(first, count)] = value.reshape(count, 8, 128)

    m_copy.wait()

    def make_products(c, carry):
        def row(y, carry):
            for m2 in range(2):
                for h in range(2):
                    px[c, 8 + y, pl.ds(m2 * 16 + h * 8, 8), :] = member(c, m2, h, y) * cz[y, pl.ds(h * 8, 8), :]
            return carry

        lax.fori_loop(0, 32, row, 0, unroll=4)
        half_blocks(c, 8, 8)
        half_blocks(c, 16, 8)
        quarter_blocks(c, 8, 8)

        @pl.when(has_n)
        def _():
            for copy in y_copies(c, 0):
                copy.start()

        @pl.when(has_s)
        def _():
            for copy in y_copies(c, 1):
                copy.start()

        return carry

    lax.fori_loop(0, CHUNKS, make_products, 0)

    low = jnp.where(has_s, 1.0, 0.0).astype(F32)
    high = jnp.where(has_n, 1.0, 0.0).astype(F32)

    def one_pass(window):
        total = window[4]
        for k in range(1, 5):
            total = total + row_taps[k] * (window[4 - k] + window[4 + k])
        return total

    def filter_rows(c, source, target, rows, fields, width, base):
        group = width // 8
        place = (lane % width) // 8

        def column(f, carry):
            at_f = pl.ds(pl.multiple_of(f * 8, 8), 8)
            window, passed = [], []
            east = west = None
            for row in range(rows):
                window.append(source[c, row, at_f, :])
                if row < 8:
                    continue
                once = one_pass(window[-9:])
                if row - 8 < 4:
                    once = once * low
                if row >= rows - 4:
                    once = once * high
                passed.append(once)
                if len(passed) < 9:
                    continue
                twice = one_pass(passed[-9:])
                y = row - 16
                target[c, y, at_f, :] = twice
                r = y % group
                to_west, to_east = roll(twice, 8 * r), roll(twice, 8 * r + 8 - width)
                if r == 0:
                    west, east = to_west, to_east
                else:
                    west, east = jnp.where(place == r, to_west, west), jnp.where(place == r, to_east, east)
                if r == group - 1:
                    start = pl.multiple_of(base + (y // group) * fields + f * 8, 8)
                    sp[0, c, pl.ds(start, 8), :] = east
                    sp[1, c, pl.ds(start, 8), :] = west
            return carry

        lax.fori_loop(0, fields // 8, column, 0)

    def rows_stage(c, carry):
        @pl.when(has_s)
        def _():
            for copy in y_copies(c, 0):
                copy.wait_recv()

        @pl.when(has_n)
        def _():
            for copy in y_copies(c, 1):
                copy.wait_recv()

        half_blocks(c, 4, 4)
        half_blocks(c, 24, 4)
        quarter_blocks(c, 4, 4)
        quarter_blocks(c, 16, 4)
        filter_rows(c, px, y1, 48, 32, 128, 0)
        filter_rows(c, p2x, y2, 32, 16, 64, 64)
        filter_rows(c, p4x, y4, 24, 8, 32, 96)

        @pl.when(has_e)
        def _():
            x_copy(c, 0).start()

        @pl.when(has_w)
        def _():
            x_copy(c, 1).start()

        return carry

    lax.fori_loop(0, CHUNKS, rows_stage, 0)

    comb[...] = jnp.zeros((32, 16, 128), F32)
    w1_copy.wait()
    w2_copy.wait()
    w4_copy.wait()

    def halo(c, start, fields, r, width):
        west, east = rp[0, c, pl.ds(start, fields), :], rp[1, c, pl.ds(start, fields), :]
        take_west = lax.broadcasted_iota(jnp.int32, (fields, 128), 1) % width < 8
        return jnp.where(take_west, roll(west, -8 * r), roll(east, 8 - 8 * r))

    def columns_stage(c, carry):
        @pl.when(has_w)
        def _():
            x_copy(c, 0).wait_recv()

        @pl.when(has_e)
        def _():
            x_copy(c, 1).wait_recv()

        sides = [halo(c, 96 + (q // 4) * 8, 8, q % 4, 32) for q in range(8)]
        value = jnp.concatenate([y4[c].reshape(64, 128), jnp.concatenate(sides, axis=0)], axis=1)
        o4[...] = full_dot(value, w4[0], w4[1])
        sides = [halo(c, 64 + (q // 8) * 16, 16, q % 8, 64) for q in range(16)]
        value = jnp.concatenate([y2[c].reshape(256, 128), jnp.concatenate(sides, axis=0)], axis=1)
        o2[...] = full_dot(value, w2[0], w2[1])

        def block(b, carry):
            for part in range(2):
                first = b * 16 + part * 8
                start = pl.multiple_of(b * 32, 32)
                sides = [halo(c, start, 32, part * 8 + r, 128) for r in range(8)]
                rows = y1[c, pl.ds(first, 8)].reshape(256, 128)
                value = full_dot(jnp.concatenate([rows, jnp.concatenate(sides, axis=0)], axis=1), w1[0], w1[1])
                for r in range(8):
                    y = first + r
                    at2 = pl.multiple_of((b * 8 + part * 4 + r // 2) * 16, 16)
                    at4 = pl.multiple_of((b * 4 + part * 2 + r // 4) * 8, 8)
                    for h in range(2):
                        total = comb[y, pl.ds(h * 8, 8), :]
                        for m2 in range(2):
                            begin = r * 32 + m2 * 16 + h * 8
                            local = value[begin : begin + 8]
                            local = local + o2[pl.ds(at2 + m2 * 8, 8), pl.ds(h * 128, 128)]
                            local = local + o4[pl.ds(at4, 8), pl.ds((m2 * 2 + h) * 128, 128)]
                            total = total + member(c, m2, h, y) * local
                        comb[y, pl.ds(h * 8, 8), :] = total
            return carry

        lax.fori_loop(0, 2, block, 0)
        return carry

    lax.fori_loop(0, CHUNKS, columns_stage, 0)

    for h in range(2):
        packed = comb[0, pl.ds(h * 8, 8), :]
        for y in range(1, 32):
            packed = jnp.where(lane == y, roll(comb[y, pl.ds(h * 8, 8), :], y), packed)
        end_col_out[pl.ds(h * 8, 8), :] = packed

    @pl.when(has_s)
    def _():
        end_row_copy.start()

    @pl.when(has_w)
    def _():
        end_col_copy.start()

    @pl.when(has_w & has_s)
    def _():
        end_corner_copy.start()

    def send_waits(c, carry):
        @pl.when(has_n)
        def _():
            for copy in y_copies(c, 0):
                copy.wait_send()

        @pl.when(has_s)
        def _():
            for copy in y_copies(c, 1):
                copy.wait_send()

        @pl.when(has_e)
        def _():
            x_copy(c, 0).wait_send()

        @pl.when(has_w)
        def _():
            x_copy(c, 1).wait_send()

        return carry

    lax.fori_loop(0, CHUNKS, send_waits, 0)

    @pl.when(has_e)
    def _():
        col_copy.wait_send()
        end_col_copy.wait_recv()

    @pl.when(has_n)
    def _():
        row_copy.wait_send()
        end_row_copy.wait_recv()

    @pl.when(has_e & has_n)
    def _():
        corner_copy.wait_send()
        end_corner_copy.wait_recv()

    extra[0] = end_row_in[...]
    extra[1] = end_col_in[...]
    extra[2] = end_corner_in[...]

    @pl.when(has_s)
    def _():
        end_row_copy.wait_send()

    @pl.when(has_w)
    def _():
        end_col_copy.wait_send()

    @pl.when(has_w & has_s)
    def _():
        end_corner_copy.wait_send()


def spread_kernel(comb, extra, spread, out_hbm, ov, sem):
    lane = lax.broadcasted_iota(jnp.int32, (16, 128), 1)
    edge = jnp.where(lane == 32, roll(extra[2], 32), extra[1])
    half_edge = 0.5 * (edge + roll(edge, -1))
    for block in range(4):
        rows = []
        for j in range(block * 8, block * 8 + 8):
            here = comb[j]
            later = comb[j + 1] if j < 31 else extra[0]
            rows.append(jnp.concatenate([here, roll(edge, -j)], axis=1))
            rows.append(jnp.concatenate([0.5 * (here + later), roll(half_edge, -j)], axis=1))
        value = exact_dot(jnp.concatenate(rows, axis=0), spread[...])
        for side in range(2):
            flat = ov.at[side].reshape(LEV * APAD, 128)
            for k in range(16):
                for h in range(2):
                    begin = k * 16 + h * 8
                    flat[pl.ds(h * 8 * APAD + block * 16 + k, 8, stride=APAD), :] = value[
                        begin : begin + 8, side * 128 : side * 128 + 128
                    ]
    copies = [
        pltpu.make_async_copy(
            ov.at[side, :, pl.ds(0, 64), :], out_hbm.at[:, :, pl.ds(side * 128, 128)], sem.at[side]
        )
        for side in range(2)
    ]
    for copy in copies:
        copy.start()
    for copy in copies:
        copy.wait()


def shards(nx, ny, gradient, members):
    filters, small, spread = constants()
    w1, w2, w4 = (jnp.asarray(value) for value in filters)
    any_space = pl.BlockSpec(memory_space=pl.ANY)
    in_vmem = pl.BlockSpec(memory_space=pltpu.VMEM)
    dma = pltpu.SemaphoreType.DMA

    def vmem(*shape, dtype=F32):
        return pltpu.VMEM(shape, dtype)

    comb, extra = pl.pallas_call(
        functools.partial(main_kernel, nx, ny),
        name="localise",
        out_shape=(jax.ShapeDtypeStruct((32, 16, 128), F32), jax.ShapeDtypeStruct((3, 16, 128), F32)),
        in_specs=[any_space] * 6,
        out_specs=(in_vmem, in_vmem),
        scratch_shapes=[
            vmem(2, LEV, 64, 128),
            vmem(MEM, LEV, MPAD, 128),
            vmem(2, 256, 128, dtype=BF16),
            vmem(2, 256, 256, dtype=BF16),
            vmem(2, 256, 512, dtype=BF16),
            vmem(2, 256, 128, dtype=BF16),
            vmem(LEV, APAD, 128),
            vmem(32, 16, 128),
            vmem(CHUNKS, 48, 32, 128),
            vmem(CHUNKS, 32, 16, 128),
            vmem(CHUNKS, 24, 8, 128),
            vmem(CHUNKS, 32, 32, 128),
            vmem(CHUNKS, 16, 16, 128),
            vmem(CHUNKS, 8, 8, 128),
            vmem(2, CHUNKS, 112, 128),
            vmem(2, CHUNKS, 112, 128),
            vmem(256, 256),
            vmem(64, 512),
            vmem(8, 128),
            vmem(8, 128),
            vmem(16, 128),
            vmem(16, 128),
            vmem(16, 128),
            vmem(16, 128),
            vmem(16, 128),
            vmem(16, 128),
            vmem(16, 128),
            vmem(16, 128),
            dma((7,)),
            dma((3,)),
            dma((3,)),
            dma((2, CHUNKS, 3)),
            dma((2, CHUNKS, 3)),
            dma((2, CHUNKS)),
            dma((2, CHUNKS)),
            dma((3,)),
            dma((3,)),
        ],
        compiler_params=pltpu.CompilerParams(collective_id=0, has_side_effects=True, vmem_limit_bytes=48 << 20),
    )(gradient, members, w1, w2, w4, jnp.asarray(small))
    return pl.pallas_call(
        spread_kernel,
        name="spread",
        out_shape=jax.ShapeDtypeStruct((LEV, 64, 256), F32),
        in_specs=[in_vmem] * 3,
        out_specs=any_space,
        scratch_shapes=[vmem(2, LEV, APAD, 128), dma((2,))],
        compiler_params=pltpu.CompilerParams(vmem_limit_bytes=16 << 20),
    )(comb, extra, jnp.asarray(spread))


def solution(mesh):
    in_specs = (P(None, "gy", "gx"), P(None, None, "gy", "gx"))
    return jax.shard_map(
        functools.partial(shards, mesh.shape["gx"], mesh.shape["gy"]),
        mesh=mesh,
        in_specs=in_specs,
        out_specs=P(None, "gy", "gx"),
        check_vma=False,
    )
```

profile of v0, /device:TPU:59, one launch (start us, length us, event | category | flops | bytes accessed | tf_op | source)
XLA Modules:
  0.0 42.0 jit_solution(11151436836772130584)
XLA Ops:
  0.0 0.0 copy-start
  0.0 1.4 %copy-done = bf16[3,2,256,512]{3,2,1,0:T(8,128)(2,1)S(1)} copy-done((bf16[3,2,256,512]{3,2,1,0:T(8,128)(2,1)S(1)}, bf16[3,2,256,512]{3,2,1,0:T(8,128)(2,1)}, u32[]{:S(2)}) %copy-start) | copy-done | bytes 1572888
  1.4 0.0 copy-start.1
  1.4 1.2 %copy-done.1 = f32[16,64,256]{2,1,0:T(8,128)S(1)} copy-done((f32[16,64,256]{2,1,0:T(8,128)S(1)}, f32[16,64,256]{2,1,0:T(8,128)}, u32[]{:S(2)}) %copy-start.1) | copy-done | bytes 1048600
  2.6 0.0 copy-start.2
  2.6 1.1 %copy-done.2 = bf16[3,2,256,256]{3,2,1,0:T(8,128)(2,1)S(1)} copy-done((bf16[3,2,256,256]{3,2,1,0:T(8,128)(2,1)S(1)}, bf16[3,2,256,256]{3,2,1,0:T(8,128)(2,1)}, u32[]{:S(2)}) %copy-start.2) | copy-done | bytes 786456
  3.8 0.0 copy-start.3
  3.8 1.0 %copy-done.3 = bf16[3,2,256,128]{3,2,1,0:T(8,128)(2,1)S(1)} copy-done((bf16[3,2,256,128]{3,2,1,0:T(8,128)(2,1)S(1)}, bf16[3,2,256,128]{3,2,1,0:T(8,128)(2,1)}, u32[]{:S(2)}) %copy-start.3) | copy-done | bytes 393240
  4.8 0.0 copy-start.4
  4.8 0.9 %copy-done.4 = bf16[2,256,128]{2,1,0:T(8,128)(2,1)S(1)} copy-done((bf16[2,256,128]{2,1,0:T(8,128)(2,1)S(1)}, bf16[2,256,128]{2,1,0:T(8,128)(2,1)}, u32[]{:S(2)}) %copy-start.4) | copy-done | bytes 131096
  5.7 0.0 copy-start.5
  5.7 34.7 %localise.1 = (f32[32,16,128]{2,1,0:T(8,128)S(1)}, f32[3,16,128]{2,1,0:T(8,128)S(1)}) custom-call(f32[16,64,256]{2,1,0:T(8,128)S(1)} %copy-done.1, f32[8,16,32,128]{3,2,1,0:T(8,128)} %m_hbm.1, bf16[3,2,256,128]{3,2,1,0:T(8,128)(2,1)S(1)} %copy-done.3, bf16[3,2,256,256]{3,2,1,0:T(8,128)(2,1)S(1)} %copy-done.2, bf16[3,2,256,512]{3,2,1,0:T(8,128)(2,1)S(1)} %copy-done, ...), custom_call_target="tpu_custom_call" | custom-call | tf_op jit(solution)/shard_map/localise/pallas_call | solution.py:580
  40.4 0.0 copy-done.5
  40.4 1.6 %spread.2 = f32[16,64,256]{2,1,0:T(8,128)} custom-call(f32[32,16,128]{2,1,0:T(8,128)S(1)} %get-tuple-element.7.comb, f32[3,16,128]{2,1,0:T(8,128)S(1)} %get-tuple-element.8.extra, bf16[256,256]{1,0:T(8,128)(2,1)S(1)} %copy-done.5), custom_call_target="tpu_custom_call" | custom-call | tf_op jit(solution)/shard_map/spread/pallas_call | solution.py:627
Async XLA Ops:
  0.0 1.4 %copy-start = (bf16[3,2,256,512]{3,2,1,0:T(8,128)(2,1)S(1)}, bf16[3,2,256,512]{3,2,1,0:T(8,128)(2,1)}, u32[]{:S(2)}) copy-start(bf16[3,2,256,512]{3,2,1,0:T(8,128)(2,1)} %constant.12.clone.w4_hbm) | copy-start | bytes 4718596
  1.4 1.2 %copy-start.1 = (f32[16,64,256]{2,1,0:T(8,128)S(1)}, f32[16,64,256]{2,1,0:T(8,128)}, u32[]{:S(2)}) copy-start(f32[16,64,256]{2,1,0:T(8,128)} %g_hbm.1) | copy-start | bytes 3145732
  2.6 1.1 %copy-start.2 = (bf16[3,2,256,256]{3,2,1,0:T(8,128)(2,1)S(1)}, bf16[3,2,256,256]{3,2,1,0:T(8,128)(2,1)}, u32[]{:S(2)}) copy-start(bf16[3,2,256,256]{3,2,1,0:T(8,128)(2,1)} %constant.11.clone.w2_hbm) | copy-start | bytes 2359300
  3.8 1.0 %copy-start.3 = (bf16[3,2,256,128]{3,2,1,0:T(8,128)(2,1)S(1)}, bf16[3,2,256,128]{3,2,1,0:T(8,128)(2,1)}, u32[]{:S(2)}) copy-start(bf16[3,2,256,128]{3,2,1,0:T(8,128)(2,1)} %constant.10.clone.w1_hbm) | copy-start | bytes 1179652
  4.8 0.9 %copy-start.4 = (bf16[2,256,128]{2,1,0:T(8,128)(2,1)S(1)}, bf16[2,256,128]{2,1,0:T(8,128)(2,1)}, u32[]{:S(2)}) copy-start(bf16[2,256,128]{2,1,0:T(8,128)(2,1)} %constant.13.clone.small_hbm) | copy-start | bytes 393220
  5.7 34.7 %copy-start.5 = (bf16[256,256]{1,0:T(8,128)(2,1)S(1)}, bf16[256,256]{1,0:T(8,128)(2,1)}, u32[]{:S(2)}) copy-start(bf16[256,256]{1,0:T(8,128)(2,1)} %constant.14.clone.spread) | copy-start | bytes 393220
where the time goes:
time: 42.5 us; the launch traced here: 42 us
  Pallas kernels  36.3 us (85%)
  local copies, waits for them, and re-layouts  5.67 us (13%)
    pallas_call x1, Pallas kernels, shards(): pl.pallas_call(functools.partial(main_kernel, nx, ny), name='localise', o...  34.7 us
    unnamed x12, local copies, waits for them, and re-layouts  5.67 us
    pallas_call x1, Pallas kernels, shards(): pl.pallas_call(spread_kernel, name='spread', out_shape=jax.ShapeDtypeStru...  1.65 us

commit v1 on v0

--- a/solution.py
+++ b/solution.py
@@ -13,6 +13,7 @@
 F32, BF16 = jnp.float32, jnp.bfloat16
 LEV, MEM = 16, 8
 CHUNKS = 4
+LAG = 2
 MPAD = 40
 APAD = 72
 
@@ -108,7 +109,7 @@
     comb, extra,
     gv, mv, w1, w2, w4, small,
     ac, cz, px, p2x, p4x, y1, y2, y4, sp, rp, o2, o4,
-    col_out, col_in, row_out, row_in, corner_out, corner_in,
+    col_out, col_in, row_out, row_in, corner_in,
     end_row_in, end_col_out, end_col_in, end_corner_in,
     local_sem, s1, r1, ys, yr, xs, xr, s3, r3,
 ):
@@ -126,7 +127,7 @@
     w1_copy = pltpu.make_async_copy(w1_hbm.at[kind], w1, local_sem.at[3])
     w2_copy = pltpu.make_async_copy(w2_hbm.at[kind], w2, local_sem.at[4])
     w4_copy = pltpu.make_async_copy(w4_hbm.at[kind], w4, local_sem.at[5])
-    for copy in (*g_copies, small_copy, m_copy, w1_copy, w2_copy, w4_copy):
+    for copy in (g_copies[1], g_copies[0], small_copy, m_copy, w1_copy, w2_copy, w4_copy):
         copy.start()
 
     barrier = pltpu.get_barrier_semaphore()
@@ -148,7 +149,7 @@
         px[:, pl.ds(0, 8)] = jnp.zeros((CHUNKS, 8, 32, 128), F32)
         p2x[:, pl.ds(0, 4)] = jnp.zeros((CHUNKS, 4, 16, 128), F32)
         p4x[:, pl.ds(0, 4)] = jnp.zeros((CHUNKS, 4, 8, 128), F32)
-        row_in[...] = jnp.zeros((16, 128), F32)
+        row_in[...] = jnp.zeros((2, 16, 128), F32)
 
     @pl.when(jnp.logical_not(has_n))
     def _():
@@ -182,22 +183,33 @@
 
     col_copy = remote(col_out, col_in, s1.at[0], r1.at[0], 1, 0)
     row_copy = remote(row_out, row_in, s1.at[1], r1.at[1], 0, 1)
-    corner_copy = remote(corner_out, corner_in, s1.at[2], r1.at[2], 1, 1)
+    corner_copy = remote(row_out.at[1], corner_in, s1.at[2], r1.at[2], 1, 1)
     end_row_copy = remote(comb.at[0], end_row_in, s3.at[0], r3.at[0], 0, -1)
     end_col_copy = remote(end_col_out, end_col_in, s3.at[1], r3.at[1], -1, 0)
     end_corner_copy = remote(end_col_out, end_corner_in, s3.at[2], r3.at[2], -1, -1)
 
-    def y_copies(c, direction):
+    def y_copies(c, direction, pieces=slice(0, 4)):
         if direction == 0:
             places = ((px, 32, 0, 8), (p2x, 16, 0, 4), (p4x, 8, 0, 4))
             dy = 1
         else:
-            places = ((px, 8, 40, 8), (p2x, 12, 28, 4), (p4x, 12, 20, 4))
+            places = ((px, 9, 41, 7), (p2x, 12, 28, 4), (p4x, 12, 20, 4), (px, 8, 40, 1))
             dy = -1
         return [
             remote(ref.at[c, pl.ds(src, n)], ref.at[c, pl.ds(dst, n)], ys.at[direction, c, i], yr.at[direction, c, i], 0, dy)
-            for i, (ref, src, dst, n) in enumerate(places)
+            for i, (ref, src, dst, n) in list(enumerate(places))[pieces]
         ]
+
+    def start_rows(c, pieces):
+        @pl.when(has_n)
+        def _():
+            for copy in y_copies(c, 0, pieces):
+                copy.start()
+
+        @pl.when(has_s)
+        def _():
+            for copy in y_copies(c, 1, pieces):
+                copy.start()
 
     def x_copy(c, direction):
         if direction == 0:
@@ -207,48 +219,43 @@
     lane = lax.broadcasted_iota(jnp.int32, (8, 128), 1)
     first_lane = lane == 0
 
-    for copy in g_copies:
-        copy.wait()
-    gr = gv.at[1].reshape(LEV * 64, 128)
+    g_copies[1].wait()
+    g0, g1 = gv.at[0].reshape(LEV * 64, 128), gv.at[1].reshape(LEV * 64, 128)
     parts = []
     for quarter in range(4):
         packed = jnp.zeros((8, 128), F32)
         for i in range(quarter * 32, quarter * 32 + 32):
-            value = gr[pl.ds(i * 8, 8), :]
-            packed = jnp.where(lane == i, roll(value, i + 1), packed)
+            packed = jnp.where(lane == i, roll(g1[pl.ds(i * 8, 8), :], i + 1), packed)
         parts.append(packed)
     col_out[...] = jnp.where(lane < 64, jnp.where(lane < 32, parts[0], parts[1]), jnp.where(lane < 96, parts[2], parts[3]))
+    pl.semaphore_wait(barrier, sum(there.astype(jnp.int32) for there, _, _ in around))
+
+    @pl.when(has_e)
+    def _():
+        col_copy.start()
+
+    g_copies[0].wait()
     for h in range(2):
-        corner_out[pl.ds(h * 8, 8), :] = gr[pl.ds(h * 8 * 64 + 63, 8, stride=64), :]
+        row_out[0, pl.ds(h * 8, 8), :] = g0[pl.ds(h * 8 * 64 + 63, 8, stride=64), :]
+        row_out[1, pl.ds(h * 8, 8), :] = g1[pl.ds(h * 8 * 64 + 63, 8, stride=64), :]
+
+    @pl.when(has_n)
+    def _():
+        row_copy.start()
+
+    @pl.when(has_e & has_n)
+    def _():
+        corner_copy.start()
 
     small_copy.wait()
-
-    def reduce_columns(l, carry):
-        ac[l, pl.ds(0, 64), :] = exact_dot(jnp.concatenate([gv[0, l], gv[1, l]], axis=1), small[1])
-        return carry
-
-    lax.fori_loop(0, LEV, reduce_columns, 0)
+    for block in range(4):
+        levels = pl.ds(block * 4, 4)
+        value = jnp.concatenate([gv[0, levels].reshape(256, 128), gv[1, levels].reshape(256, 128)], axis=1)
+        ac[levels, pl.ds(0, 64), :] = exact_dot(value, small[1]).reshape(4, 64, 128)
     ar = ac.reshape(LEV * APAD, 128)
 
     def across_row(y, h):
         return ar[pl.ds(h * 8 * APAD + y, 8, stride=APAD), :]
-
-    for h in range(2):
-        row_out[pl.ds(h * 8, 8), :] = across_row(63, h)
-
-    pl.semaphore_wait(barrier, sum(there.astype(jnp.int32) for there, _, _ in around))
-
-    @pl.when(has_e)
-    def _():
-        col_copy.start()
-
-    @pl.when(has_n)
-    def _():
-        row_copy.start()
-
-    @pl.when(has_e & has_n)
-    def _():
-        corner_copy.start()
 
     @pl.when(has_w)
     def _():
@@ -258,19 +265,6 @@
             for block in range(8):
                 tile = ac[l, pl.ds(block * 8, 8), :]
                 ac[l, pl.ds(block * 8, 8), :] = tile + jnp.where(first_lane, roll(value, -(l * 8 + block)), 0.0)
-
-    @pl.when(has_s)
-    def _():
-        row_copy.wait_recv()
-
-    @pl.when(has_w & has_s)
-    def _():
-        corner_copy.wait_recv()
-
-    before = []
-    for h in range(2):
-        corner = corner_in[pl.ds(h * 8, 8), :]
-        before.append(row_in[pl.ds(h * 8, 8), :] + jnp.where(first_lane, 0.5 * roll(corner, 1), 0.0))
 
     def reduce_rows(j, carry):
         odd_rows = []
@@ -280,7 +274,7 @@
             odd_rows.append(odd)
         return tuple(odd_rows)
 
-    lax.fori_loop(0, 32, reduce_rows, tuple(before))
+    lax.fori_loop(1, 32, reduce_rows, tuple(across_row(1, h) for h in range(2)))
 
     mr = mv.reshape(MEM * LEV * MPAD, 128)
 
@@ -306,31 +300,52 @@
 
     m_copy.wait()
 
+    def product_row(c, y):
+        for m2 in range(2):
+            for h in range(2):
+                px[c, 8 + y, pl.ds(m2 * 16 + h * 8, 8), :] = member(c, m2, h, y) * cz[y, pl.ds(h * 8, 8), :]
+
+    def product_rows(c):
+        def row(y, carry):
+            product_row(c, y)
+            return carry
+
+        lax.fori_loop(1, 32, row, 0, unroll=4)
+
+    early, late = slice(0, 2), slice(2, 4)
+    product_rows(0)
+    half_blocks(0, 12, 8)
+    start_rows(0, early)
+
+    @pl.when(has_s)
+    def _():
+        row_copy.wait_recv()
+
+    @pl.when(has_w & has_s)
+    def _():
+        corner_copy.wait_recv()
+
+    before = exact_dot(jnp.concatenate([row_in[0], row_in[1]], axis=1), small[1])
+    for h in range(2):
+        corner = jnp.where(first_lane, 0.5 * roll(corner_in[pl.ds(h * 8, 8), :], 1), 0.0)
+        earlier = before[h * 8 : h * 8 + 8] + corner
+        cz[0, pl.ds(h * 8, 8), :] = across_row(0, h) + 0.5 * (across_row(1, h) + earlier)
+    for c in range(CHUNKS):
+        product_row(c, 0)
+    half_blocks(0, 8, 4)
+    half_blocks(0, 20, 4)
+    quarter_blocks(0, 8, 8)
+    start_rows(0, late)
+
     def make_products(c, carry):
-        def row(y, carry):
-            for m2 in range(2):
-                for h in range(2):
-                    px[c, 8 + y, pl.ds(m2 * 16 + h * 8, 8), :] = member(c, m2, h, y) * cz[y, pl.ds(h * 8, 8), :]
-            return carry
-
-        lax.fori_loop(0, 32, row, 0, unroll=4)
+        product_rows(c)
         half_blocks(c, 8, 8)
         half_blocks(c, 16, 8)
         quarter_blocks(c, 8, 8)
-
-        @pl.when(has_n)
-        def _():
-            for copy in y_copies(c, 0):
-                copy.start()
-
-        @pl.when(has_s)
-        def _():
-            for copy in y_copies(c, 1):
-                copy.start()
-
+        start_rows(c, slice(0, 4))
         return carry
 
-    lax.fori_loop(0, CHUNKS, make_products, 0)
+    lax.fori_loop(1, CHUNKS, make_products, 0)
 
     low = jnp.where(has_s, 1.0, 0.0).astype(F32)
     high = jnp.where(has_n, 1.0, 0.0).astype(F32)
@@ -378,7 +393,7 @@
 
         lax.fori_loop(0, fields // 8, column, 0)
 
-    def rows_stage(c, carry):
+    def rows_stage(c):
         @pl.when(has_s)
         def _():
             for copy in y_copies(c, 0):
@@ -405,10 +420,6 @@
         def _():
             x_copy(c, 1).start()
 
-        return carry
-
-    lax.fori_loop(0, CHUNKS, rows_stage, 0)
-
     comb[...] = jnp.zeros((32, 16, 128), F32)
     w1_copy.wait()
     w2_copy.wait()
@@ -419,7 +430,7 @@
         take_west = lax.broadcasted_iota(jnp.int32, (fields, 128), 1) % width < 8
         return jnp.where(take_west, roll(west, -8 * r), roll(east, 8 - 8 * r))
 
-    def columns_stage(c, carry):
+    def columns_stage(c):
         @pl.when(has_w)
         def _():
             x_copy(c, 0).wait_recv()
@@ -458,9 +469,19 @@
             return carry
 
         lax.fori_loop(0, 2, block, 0)
+
+    def stages(step, carry):
+        @pl.when(step < CHUNKS)
+        def _():
+            rows_stage(step)
+
+        @pl.when(step >= LAG)
+        def _():
+            columns_stage(step - LAG)
+
         return carry
 
-    lax.fori_loop(0, CHUNKS, columns_stage, 0)
+    lax.fori_loop(0, CHUNKS + LAG, stages, 0)
 
     for h in range(2):
         packed = comb[0, pl.ds(h * 8, 8), :]
@@ -570,7 +591,7 @@
 def shards(nx, ny, gradient, members):
     filters, small, spread = constants()
     w1, w2, w4 = (jnp.asarray(value) for value in filters)
-    any_space = pl.BlockSpec(memory_space=pl.ANY)
+    any_space = pl.BlockSpec(memory_space=pltpu.HBM)
     in_vmem = pl.BlockSpec(memory_space=pltpu.VMEM)
     dma = pltpu.SemaphoreType.DMA
 
@@ -604,9 +625,8 @@
             vmem(64, 512),
             vmem(8, 128),
             vmem(8, 128),
-            vmem(16, 128),
-            vmem(16, 128),
-            vmem(16, 128),
+            vmem(2, 16, 128),
+            vmem(2, 16, 128),
             vmem(16, 128),
             vmem(16, 128),
             vmem(16, 128),
@@ -615,15 +635,15 @@
             dma((7,)),
             dma((3,)),
             dma((3,)),
-            dma((2, CHUNKS, 3)),
-            dma((2, CHUNKS, 3)),
+            dma((2, CHUNKS, 4)),
+            dma((2, CHUNKS, 4)),
             dma((2, CHUNKS)),
             dma((2, CHUNKS)),
             dma((3,)),
             dma((3,)),
         ],
         compiler_params=pltpu.CompilerParams(collective_id=0, has_side_effects=True, vmem_limit_bytes=48 << 20),
-    )(gradient, members, w1, w2, w4, jnp.asarray(small))
+    )(*(pltpu.with_memory_space_constraint(value, pltpu.HBM) for value in (gradient, members, w1, w2, w4, jnp.asarray(small))))
     return pl.pallas_call(
         spread_kernel,
         name="spread",

time: 42.5 us -> 35.8 us (0.84)
  local copies, waits for them, and re-layouts: 5.67 us -> 0.01 us
  Pallas kernels: 36.3 us -> 35.7 us
    unnamed x12 -> x2, local copies, waits for them, and re-layouts: 5.67 us -> 0.01 us
    pallas_call x1, Pallas kernels: 34.7 us -> 34.1 us  [shards(): pl.pallas_call(functools.partial(main_kernel, nx, ny), name='localise', o...]
where the time goes in v1:
time: 35.8 us; the launch traced here: 35.7 us
  Pallas kernels  35.7 us (100%)
    pallas_call x1, Pallas kernels, shards(): pl.pallas_call(functools.partial(main_kernel, nx, ny), name='localise', o...  34.1 us
    pallas_call x1, Pallas kernels, shards(): pl.pallas_call(spread_kernel, name='spread', out_shape=jax.ShapeDtypeStru...  1.65 us

profile of v1, /device:TPU:59, one launch (start us, length us, event | category | flops | bytes accessed | tf_op | source)
XLA Modules:
  0.0 35.7 jit_solution(11962566140874561477)
XLA Ops:
  0.0 0.0 copy-start
  0.0 34.1 %localise.1 = (f32[32,16,128]{2,1,0:T(8,128)S(1)}, f32[3,16,128]{2,1,0:T(8,128)S(1)}) custom-call(f32[16,64,256]{2,1,0:T(8,128)} %g_hbm.1, f32[8,16,32,128]{3,2,1,0:T(8,128)} %m_hbm.1, bf16[3,2,256,128]{3,2,1,0:T(8,128)(2,1)} %constant.10.clone.w1_hbm, bf16[3,2,256,256]{3,2,1,0:T(8,128)(2,1)} %constant.11.clone.w2_hbm, ...), custom_call_target="tpu_custom_call" | custom-call | tf_op jit(solution)/shard_map/localise/pallas_call | solution.py:601
  34.1 0.0 copy-done
  34.1 1.6 %spread.2 = f32[16,64,256]{2,1,0:T(8,128)} custom-call(f32[32,16,128]{2,1,0:T(8,128)S(1)} %get-tuple-element.7.comb, f32[3,16,128]{2,1,0:T(8,128)S(1)} %get-tuple-element.8.extra, bf16[256,256]{1,0:T(8,128)(2,1)S(1)} %copy-done), custom_call_target="tpu_custom_call" | custom-call | tf_op jit(solution)/shard_map/spread/pallas_call | solution.py:647
Async XLA Ops:
  0.0 34.1 %copy-start = (bf16[256,256]{1,0:T(8,128)(2,1)S(1)}, bf16[256,256]{1,0:T(8,128)(2,1)}, u32[]{:S(2)}) copy-start(bf16[256,256]{1,0:T(8,128)(2,1)} %constant.14.clone.spread) | copy-start | bytes 393220

commit v2 on v1

--- a/solution.py
+++ b/solution.py
@@ -55,11 +55,31 @@
     return halves(result)
 
 
+def row_filter(south_edge, north_edge):
+    result = np.zeros((96, 128))
+    start = 0
+    for factor, _ in generations:
+        count = 32 // factor
+        inside = np.ones(count + 8)
+        if south_edge:
+            inside[:4] = 0.0
+        if north_edge:
+            inside[-4:] = 0.0
+        both = band(count + 8) @ (inside[:, None] * band(count)) / beta_taps[4] ** 2
+        for row in range(96):
+            block = (row - 32) // factor + 8
+            if 0 <= block < count + 16:
+                result[row, start : start + count] = both[block]
+        start += count
+    return halves(result)
+
+
 def constants():
     filters = []
     for factor, weight in generations:
         kinds = [column_filter(factor, weight, *edges) for edges in ((True, False), (False, False), (False, True))]
         filters.append(np.stack(kinds))
+    filters[0] = np.concatenate([filters[0][:, 0], filters[0][:, 1]], axis=2)
     pairs = np.zeros((256, 128))
     reduce_columns = np.zeros((256, 128))
     for lane in range(128):
@@ -68,13 +88,25 @@
         reduce_columns[2 * lane + 1, lane] = 0.5
         if lane:
             reduce_columns[2 * lane - 1, lane] = 0.5
-    small = np.stack([pairs, reduce_columns]).astype(ml_dtypes.bfloat16)
+    fours = np.zeros((2, 256, 128))
+    for lane in range(256):
+        fours[0, lane, lane // 4] = 1.0
+        fours[1, lane, 64 + lane // 4] = 1.0
+    border = np.zeros((256, 128))
+    for chunk in range(CHUNKS):
+        for j in range(32):
+            border[2 * j, chunk * 32 + j] = 0.5
+            border[2 * j + 1, chunk * 32 + j] = 0.25
+            if j:
+                border[2 * j - 1, chunk * 32 + j] = 0.25
+    small = np.stack([pairs, reduce_columns, *fours, border]).astype(ml_dtypes.bfloat16)
+    rows = np.stack([row_filter(*edges) for edges in ((True, False), (False, False), (False, True))])
     spread = np.zeros((256, 256))
     for lane in range(128):
         spread[lane, 2 * lane] = 1.0
         spread[lane, 2 * lane + 1] = 0.5
         spread[lane + 1, 2 * lane + 1] = 0.5
-    return filters, small, spread.astype(ml_dtypes.bfloat16)
+    return filters, rows, small, spread.astype(ml_dtypes.bfloat16)
 
 
 def split(value):
@@ -105,13 +137,13 @@
 
 def main_kernel(
     nx, ny,
-    g_hbm, m_hbm, w1_hbm, w2_hbm, w4_hbm, small_hbm,
+    g_hbm, m_hbm, w1_hbm, w2_hbm, w4_hbm, wr_hbm, small_hbm,
     comb, extra,
-    gv, mv, w1, w2, w4, small,
+    gv, mv, w1, w2, w4, wr, small,
     ac, cz, px, p2x, p4x, y1, y2, y4, sp, rp, o2, o4,
-    col_out, col_in, row_out, row_in, corner_in,
+    col_out, col_in, row_out, row_in, corner_in, m_out, m_in, c_out, c_in, dp, dp_in, add_rows, a1, a2, a4,
     end_row_in, end_col_out, end_col_in, end_corner_in,
-    local_sem, s1, r1, ys, yr, xs, xr, s3, r3,
+    local_sem, wr_sem, s1, r1, sf, rf, ys, yr, xs, xr, s3, r3,
 ):
     gx, gy = lax.axis_index("gx"), lax.axis_index("gy")
     has_w, has_e = gx > 0, gx < nx - 1
@@ -119,7 +151,9 @@
 
     kind = 1 - (gx == 0).astype(jnp.int32) + (gx == nx - 1).astype(jnp.int32)
     g_copies = [
-        pltpu.make_async_copy(g_hbm.at[:, :, pl.ds(side * 128, 128)], gv.at[side], local_sem.at[side * 6])
+        pltpu.make_async_copy(
+            g_hbm.at[:, :, pl.ds(side * 128, 128)], gv.at[side, :, pl.ds(0, 64), :], local_sem.at[side * 6]
+        )
         for side in range(2)
     ]
     m_copy = pltpu.make_async_copy(m_hbm, mv.at[:, :, pl.ds(0, 32), :], local_sem.at[1])
@@ -127,7 +161,16 @@
     w1_copy = pltpu.make_async_copy(w1_hbm.at[kind], w1, local_sem.at[3])
     w2_copy = pltpu.make_async_copy(w2_hbm.at[kind], w2, local_sem.at[4])
     w4_copy = pltpu.make_async_copy(w4_hbm.at[kind], w4, local_sem.at[5])
-    for copy in (g_copies[1], g_copies[0], small_copy, m_copy, w1_copy, w2_copy, w4_copy):
+    row_kind = 1 - (gy == 0).astype(jnp.int32) + (gy == ny - 1).astype(jnp.int32)
+    wr_copies = [
+        pltpu.make_async_copy(
+            wr_hbm.at[row_kind, part, pl.ds(tile * 32, 32), :],
+            wr.at[part, tile, pl.ds(c * 32, 32), pl.ds(c * 128, 128)],
+            wr_sem.at[part, tile, c],
+        )
+        for part in range(2) for tile in range(3) for c in range(CHUNKS)
+    ]
+    for copy in (g_copies[1], g_copies[0], small_copy, m_copy, *wr_copies, w1_copy, w2_copy, w4_copy):
         copy.start()
 
     barrier = pltpu.get_barrier_semaphore()
@@ -144,12 +187,20 @@
         def _(dx=dx, dy=dy):
             pl.semaphore_signal(barrier, inc=1, device_id=at(dx, dy), device_id_type=MESH)
 
+    for part in range(2):
+        for tile in range(3):
+            for c in range(CHUNKS):
+                for other in range(CHUNKS):
+                    if other != c:
+                        wr[part, tile, pl.ds(c * 32, 32), pl.ds(other * 128, 128)] = jnp.zeros((32, 128), BF16)
+
     @pl.when(jnp.logical_not(has_s))
     def _():
         px[:, pl.ds(0, 8)] = jnp.zeros((CHUNKS, 8, 32, 128), F32)
         p2x[:, pl.ds(0, 4)] = jnp.zeros((CHUNKS, 4, 16, 128), F32)
         p4x[:, pl.ds(0, 4)] = jnp.zeros((CHUNKS, 4, 8, 128), F32)
         row_in[...] = jnp.zeros((2, 16, 128), F32)
+        dp_in[0] = jnp.zeros((32, 128), F32)
 
     @pl.when(jnp.logical_not(has_n))
     def _():
@@ -157,11 +208,12 @@
         p2x[:, pl.ds(28, 4)] = jnp.zeros((CHUNKS, 4, 16, 128), F32)
         p4x[:, pl.ds(20, 4)] = jnp.zeros((CHUNKS, 4, 8, 128), F32)
         end_row_in[...] = jnp.zeros((16, 128), F32)
+        dp_in[1] = jnp.zeros((32, 128), F32)
 
     @pl.when(jnp.logical_not(has_w))
     def _():
         rp[0] = jnp.zeros((CHUNKS, 112, 128), F32)
-        col_in[...] = jnp.zeros((8, 128), F32)
+        col_in[...] = jnp.zeros((16, 128), F32)
 
     @pl.when(jnp.logical_not(has_e))
     def _():
@@ -183,33 +235,27 @@
 
     col_copy = remote(col_out, col_in, s1.at[0], r1.at[0], 1, 0)
     row_copy = remote(row_out, row_in, s1.at[1], r1.at[1], 0, 1)
-    corner_copy = remote(row_out.at[1], corner_in, s1.at[2], r1.at[2], 1, 1)
+    corner_copy = remote(col_out, corner_in, s1.at[2], r1.at[2], 1, 1)
     end_row_copy = remote(comb.at[0], end_row_in, s3.at[0], r3.at[0], 0, -1)
     end_col_copy = remote(end_col_out, end_col_in, s3.at[1], r3.at[1], -1, 0)
-    end_corner_copy = remote(end_col_out, end_corner_in, s3.at[2], r3.at[2], -1, -1)
-
-    def y_copies(c, direction, pieces=slice(0, 4)):
+    end_corner_copy = remote(comb.at[0], end_corner_in, s3.at[2], r3.at[2], -1, -1)
+
+    def y_copies(c, direction, pieces=slice(0, 3)):
         if direction == 0:
             places = ((px, 32, 0, 8), (p2x, 16, 0, 4), (p4x, 8, 0, 4))
             dy = 1
         else:
-            places = ((px, 9, 41, 7), (p2x, 12, 28, 4), (p4x, 12, 20, 4), (px, 8, 40, 1))
+            places = ((px, 9, 41, 7), (p2x, 12, 28, 4), (p4x, 12, 20, 4))
             dy = -1
         return [
             remote(ref.at[c, pl.ds(src, n)], ref.at[c, pl.ds(dst, n)], ys.at[direction, c, i], yr.at[direction, c, i], 0, dy)
             for i, (ref, src, dst, n) in list(enumerate(places))[pieces]
         ]
 
-    def start_rows(c, pieces):
-        @pl.when(has_n)
-        def _():
-            for copy in y_copies(c, 0, pieces):
-                copy.start()
-
-        @pl.when(has_s)
-        def _():
-            for copy in y_copies(c, 1, pieces):
-                copy.start()
+    first_members = remote(m_out, m_in, sf.at[0], rf.at[0], 0, -1)
+    dp_north = remote(dp, dp_in.at[0], sf.at[2], rf.at[2], 0, 1)
+    dp_south = remote(dp, dp_in.at[1], sf.at[3], rf.at[3], 0, -1)
+    first_coarse = remote(c_out, c_in, sf.at[1], rf.at[1], 0, -1)
 
     def x_copy(c, direction):
         if direction == 0:
@@ -220,51 +266,56 @@
     first_lane = lane == 0
 
     g_copies[1].wait()
-    g0, g1 = gv.at[0].reshape(LEV * 64, 128), gv.at[1].reshape(LEV * 64, 128)
-    parts = []
-    for quarter in range(4):
-        packed = jnp.zeros((8, 128), F32)
-        for i in range(quarter * 32, quarter * 32 + 32):
-            packed = jnp.where(lane == i, roll(g1[pl.ds(i * 8, 8), :], i + 1), packed)
-        parts.append(packed)
-    col_out[...] = jnp.where(lane < 64, jnp.where(lane < 32, parts[0], parts[1]), jnp.where(lane < 96, parts[2], parts[3]))
-    pl.semaphore_wait(barrier, sum(there.astype(jnp.int32) for there, _, _ in around))
-
-    @pl.when(has_e)
-    def _():
-        col_copy.start()
-
+    g0, g1 = gv.at[0].reshape(LEV * APAD, 128), gv.at[1].reshape(LEV * APAD, 128)
+
+    def gradient_row(half, y, h):
+        return half[pl.ds(h * 8 * APAD + y, 8, stride=APAD), :]
+
+    for h in range(2):
+        parts = []
+        for quarter in range(2):
+            packed = jnp.zeros((8, 128), F32)
+            for y in range(quarter * 32, quarter * 32 + 32):
+                packed = jnp.where(lane == y, roll(gradient_row(g1, y, h), y + 1), packed)
+            parts.append(packed)
+        col_out[pl.ds(h * 8, 8), :] = jnp.where(lane < 32, parts[0], parts[1])
     g_copies[0].wait()
     for h in range(2):
-        row_out[0, pl.ds(h * 8, 8), :] = g0[pl.ds(h * 8 * 64 + 63, 8, stride=64), :]
-        row_out[1, pl.ds(h * 8, 8), :] = g1[pl.ds(h * 8 * 64 + 63, 8, stride=64), :]
-
-    @pl.when(has_n)
-    def _():
-        row_copy.start()
-
-    @pl.when(has_e & has_n)
-    def _():
-        corner_copy.start()
+        row_out[0, pl.ds(h * 8, 8), :] = gradient_row(g0, 63, h)
+        row_out[1, pl.ds(h * 8, 8), :] = gradient_row(g1, 63, h)
 
     small_copy.wait()
     for block in range(4):
         levels = pl.ds(block * 4, 4)
-        value = jnp.concatenate([gv[0, levels].reshape(256, 128), gv[1, levels].reshape(256, 128)], axis=1)
+        value = jnp.concatenate(
+            [gv[side, levels, pl.ds(0, 64), :].reshape(256, 128) for side in range(2)], axis=1
+        )
         ac[levels, pl.ds(0, 64), :] = exact_dot(value, small[1]).reshape(4, 64, 128)
     ar = ac.reshape(LEV * APAD, 128)
 
     def across_row(y, h):
         return ar[pl.ds(h * 8 * APAD + y, 8, stride=APAD), :]
 
-    @pl.when(has_w)
-    def _():
-        col_copy.wait_recv()
-        value = 0.5 * col_in[...]
-        for l in range(LEV):
-            for block in range(8):
-                tile = ac[l, pl.ds(block * 8, 8), :]
-                ac[l, pl.ds(block * 8, 8), :] = tile + jnp.where(first_lane, roll(value, -(l * 8 + block)), 0.0)
+    for h in range(2):
+        c_out[pl.ds(h * 8, 8), :] = across_row(0, h) + 0.5 * across_row(1, h)
+
+    pl.semaphore_wait(barrier, sum(there.astype(jnp.int32) for there, _, _ in around))
+
+    @pl.when(has_e)
+    def _():
+        col_copy.start()
+
+    @pl.when(has_n)
+    def _():
+        row_copy.start()
+
+    @pl.when(has_e & has_n)
+    def _():
+        corner_copy.start()
+
+    @pl.when(has_s)
+    def _():
+        first_coarse.start()
 
     def reduce_rows(j, carry):
         odd_rows = []
@@ -275,77 +326,210 @@
         return tuple(odd_rows)
 
     lax.fori_loop(1, 32, reduce_rows, tuple(across_row(1, h) for h in range(2)))
-
     mr = mv.reshape(MEM * LEV * MPAD, 128)
 
     def member(c, m2, h, y):
         return mr[pl.ds(((2 * c + m2) * LEV + h * 8) * MPAD + y, 8, stride=MPAD), :]
 
-    def half_blocks(c, first, count):
+    m_copy.wait()
+
+    def half_blocks(places):
         rows = []
-        for k in range(count):
-            pair = px[c, 2 * (first + k) - 8] + px[c, 2 * (first + k) - 7]
+        for c, k in places:
+            pair = px[c, 2 * k - 8] + px[c, 2 * k - 7]
             for m2 in range(2):
                 rows.append(jnp.concatenate([pair[m2 * 16 : m2 * 16 + 8], pair[m2 * 16 + 8 : m2 * 16 + 16]], axis=1))
         value = exact_dot(jnp.concatenate(rows, axis=0), small[0])
-        p2x[c, pl.ds(first, count)] = value.reshape(count, 16, 128)
-
-    def quarter_blocks(c, first, count):
+        for i, (c, k) in enumerate(places):
+            p2x[c, k] = value[i * 16 : i * 16 + 16]
+
+    def quarter_blocks(places):
         rows = []
-        for k in range(count):
-            pair = p2x[c, 2 * (first + k) - 8] + p2x[c, 2 * (first + k) - 7]
+        for c, k in places:
+            pair = p2x[c, 2 * k - 8] + p2x[c, 2 * k - 7]
             rows.append(jnp.concatenate([pair[:8], pair[8:]], axis=1))
         value = exact_dot(jnp.concatenate(rows, axis=0), small[0])
-        p4x[c, pl.ds(first, count)] = value.reshape(count, 8, 128)
-
-    m_copy.wait()
+        for i, (c, k) in enumerate(places):
+            p4x[c, k] = value[i * 8 : i * 8 + 8]
+
+    def quarter_blocks_of_rows(places):
+        rows = [[], []]
+        for c, k, row in places:
+            four = (px[c, row] + px[c, row + 1]) + (px[c, row + 2] + px[c, row + 3])
+            for m2 in range(2):
+                rows[m2].append(jnp.concatenate([four[m2 * 16 : m2 * 16 + 8], four[m2 * 16 + 8 : m2 * 16 + 16]], axis=1))
+        value = sum(exact_dot(jnp.concatenate(rows[m2], axis=0), small[2 + m2]) for m2 in range(2))
+        for i, (c, k, _) in enumerate(places):
+            p4x[c, k] = value[i * 8 : i * 8 + 8]
 
     def product_row(c, y):
         for m2 in range(2):
             for h in range(2):
                 px[c, 8 + y, pl.ds(m2 * 16 + h * 8, 8), :] = member(c, m2, h, y) * cz[y, pl.ds(h * 8, 8), :]
 
-    def product_rows(c):
+    def start_rows(c, north, south):
+        @pl.when(has_n)
+        def _():
+            for copy in y_copies(c, 0, north):
+                copy.start()
+
+        @pl.when(has_s)
+        def _():
+            for copy in y_copies(c, 1, south):
+                copy.start()
+
+    everything, nothing = slice(0, 3), slice(0, 0)
+
+    def later_rows(c):
         def row(y, carry):
             product_row(c, y)
             return carry
 
         lax.fori_loop(1, 32, row, 0, unroll=4)
 
-    early, late = slice(0, 2), slice(2, 4)
-    product_rows(0)
-    half_blocks(0, 12, 8)
-    start_rows(0, early)
+    def first_columns():
+        @pl.when(has_w)
+        def _():
+            col_copy.wait_recv()
+
+        coarse = exact_dot(jnp.concatenate([col_in[...], jnp.zeros((16, 128), F32)], axis=1), small[4])
+
+        for m2 in range(2):
+            for h in range(2):
+                columns = []
+                for c in range(CHUNKS):
+                    column = roll(member(c, m2, h, 0), c * 32)
+                    for y in range(1, 32):
+                        place = c * 32 + y
+                        column = jnp.where(lane == place, roll(member(c, m2, h, y), place), column)
+                    columns.append(column)
+                column = columns[0]
+                for c in range(1, CHUNKS):
+                    column = jnp.where(lane >= c * 32, columns[c], column)
+                dp[pl.ds(m2 * 16 + h * 8, 8), :] = column * coarse[h * 8 : h * 8 + 8]
+
+        @pl.when(has_n)
+        def _():
+            dp_north.start()
+
+        @pl.when(has_s)
+        def _():
+            dp_south.start()
+
+    def without_first_row(c, carry):
+        later_rows(c)
+        half_blocks([(c, k) for k in range(12, 24)])
+        quarter_blocks([(c, k) for k in range(12, 16)])
+        start_rows(c, slice(0, 2), everything)
+        return carry
+
+    def first_row(c, carry):
+        product_row(c, 0)
+        half_blocks([(c, k) for k in range(8, 12)])
+        quarter_blocks([(c, k) for k in range(8, 12)])
+        start_rows(c, slice(2, 3), nothing)
+        return carry
+
+    def whole(c, carry):
+        later_rows(c)
+        product_row(c, 0)
+        half_blocks([(c, k) for k in range(8, 24)])
+        quarter_blocks([(c, k) for k in range(8, 16)])
+        start_rows(c, everything, everything)
+        return carry
+
+    def first_coarse_row():
+        @pl.when(has_s)
+        def _():
+            row_copy.wait_recv()
+
+        @pl.when(has_w & has_s)
+        def _():
+            corner_copy.wait_recv()
+
+        before = exact_dot(jnp.concatenate([row_in[0], row_in[1]], axis=1), small[1])
+        for h in range(2):
+            corner = jnp.where(first_lane, 0.5 * roll(corner_in[pl.ds(h * 8, 8), :], -63), 0.0)
+            cz[0, pl.ds(h * 8, 8), :] = c_out[pl.ds(h * 8, 8), :] + 0.5 * (before[h * 8 : h * 8 + 8] + corner)
+
+    far = (gy % 8 == 0) & has_s
+    without_first_row(0, 0)
 
     @pl.when(has_s)
     def _():
-        row_copy.wait_recv()
-
-    @pl.when(has_w & has_s)
-    def _():
-        corner_copy.wait_recv()
-
-    before = exact_dot(jnp.concatenate([row_in[0], row_in[1]], axis=1), small[1])
-    for h in range(2):
-        corner = jnp.where(first_lane, 0.5 * roll(corner_in[pl.ds(h * 8, 8), :], 1), 0.0)
-        earlier = before[h * 8 : h * 8 + 8] + corner
-        cz[0, pl.ds(h * 8, 8), :] = across_row(0, h) + 0.5 * (across_row(1, h) + earlier)
+        for c in range(CHUNKS):
+            for m2 in range(2):
+                for h in range(2):
+                    m_out[c, pl.ds(m2 * 16 + h * 8, 8), :] = member(c, m2, h, 0)
+        first_members.start()
+
+    far_west = (gx % 4 == 0) & has_w
+
+    @pl.when(far_west)
+    def _():
+        without_first_row(1, 0)
+
+    first_columns()
+
+    @pl.when(jnp.logical_not(far_west))
+    def _():
+        without_first_row(1, 0)
+
+    @pl.when(far)
+    def _():
+        lax.fori_loop(2, CHUNKS, without_first_row, 0)
+
+    first_coarse_row()
+
+    @pl.when(far)
+    def _():
+        lax.fori_loop(0, CHUNKS, first_row, 0)
+
+    @pl.when(jnp.logical_not(far))
+    def _():
+        lax.fori_loop(0, 2, first_row, 0)
+        lax.fori_loop(2, CHUNKS, whole, 0)
+
+    @pl.when(has_n)
+    def _():
+        first_members.wait_recv()
+        first_coarse.wait_recv()
+        for h in range(2):
+            corner = jnp.where(first_lane, 0.5 * roll(col_in[pl.ds(h * 8, 8), :], -63), 0.0)
+            coarse = c_in[pl.ds(h * 8, 8), :] + 0.5 * (across_row(63, h) + corner)
+            for c in range(CHUNKS):
+                for m2 in range(2):
+                    at_f = pl.ds(m2 * 16 + h * 8, 8)
+                    px[c, 40, at_f, :] = m_in[c, at_f, :] * coarse
+
+    @pl.when(has_s)
+    def _():
+        dp_north.wait_recv()
+
+    @pl.when(has_n)
+    def _():
+        dp_south.wait_recv()
+
+    for copy in wr_copies:
+        copy.wait()
+    columns = jnp.concatenate([dp_in[0], dp[...], dp_in[1]], axis=1)
+    hi, lo = split(columns)
+    weights = [wr[part].reshape(384, 512) for part in range(2)]
+    value = dot(jnp.concatenate([hi, lo], axis=0), weights[0])
+    value = value[:32] + value[32:] + dot(hi, weights[1])
     for c in range(CHUNKS):
-        product_row(c, 0)
-    half_blocks(0, 8, 4)
-    half_blocks(0, 20, 4)
-    quarter_blocks(0, 8, 8)
-    start_rows(0, late)
-
-    def make_products(c, carry):
-        product_rows(c)
-        half_blocks(c, 8, 8)
-        half_blocks(c, 16, 8)
-        quarter_blocks(c, 8, 8)
-        start_rows(c, slice(0, 4))
-        return carry
-
-    lax.fori_loop(1, CHUNKS, make_products, 0)
+        add_rows[c] = value[:, c * 128 : c * 128 + 128]
+
+    def spread_additions(c):
+        for target, rows, width, first in ((a1, 32, 128, 0), (a2, 16, 64, 32), (a4, 8, 32, 48)):
+            parts = 128 // width
+            for f in range(4 // parts):
+                fields = [add_rows[c, pl.ds((f * parts + part) * 8, 8), :] for part in range(parts)]
+                for y in range(rows):
+                    add = jnp.zeros((8, 128), F32)
+                    for part in range(parts):
+                        add = jnp.where(lane == part * width, roll(fields[part], part * width - first - y), add)
+                    target[c, y, pl.ds(f * 8, 8), :] = add
 
     low = jnp.where(has_s, 1.0, 0.0).astype(F32)
     high = jnp.where(has_n, 1.0, 0.0).astype(F32)
@@ -356,12 +540,12 @@
             total = total + row_taps[k] * (window[4 - k] + window[4 + k])
         return total
 
-    def filter_rows(c, source, target, rows, fields, width, base):
+    def filter_rows(c, source, target, rows, fields, width, base, additions):
         group = width // 8
         place = (lane % width) // 8
 
         def column(f, carry):
-            at_f = pl.ds(pl.multiple_of(f * 8, 8), 8)
+            at_f = pl.ds(f * 8, 8)
             window, passed = [], []
             east = west = None
             for row in range(rows):
@@ -378,6 +562,7 @@
                     continue
                 twice = one_pass(passed[-9:])
                 y = row - 16
+                twice = twice + additions[c, y, at_f, :]
                 target[c, y, at_f, :] = twice
                 r = y % group
                 to_west, to_east = roll(twice, 8 * r), roll(twice, 8 * r + 8 - width)
@@ -386,14 +571,17 @@
                 else:
                     west, east = jnp.where(place == r, to_west, west), jnp.where(place == r, to_east, east)
                 if r == group - 1:
-                    start = pl.multiple_of(base + (y // group) * fields + f * 8, 8)
+                    start = base + (y // group) * fields + f * 8
                     sp[0, c, pl.ds(start, 8), :] = east
                     sp[1, c, pl.ds(start, 8), :] = west
             return carry
 
-        lax.fori_loop(0, fields // 8, column, 0)
+        for f in range(fields // 8):
+            column(f, 0)
 
     def rows_stage(c):
+        spread_additions(c)
+
         @pl.when(has_s)
         def _():
             for copy in y_copies(c, 0):
@@ -404,13 +592,12 @@
             for copy in y_copies(c, 1):
                 copy.wait_recv()
 
-        half_blocks(c, 4, 4)
-        half_blocks(c, 24, 4)
-        quarter_blocks(c, 4, 4)
-        quarter_blocks(c, 16, 4)
-        filter_rows(c, px, y1, 48, 32, 128, 0)
-        filter_rows(c, p2x, y2, 32, 16, 64, 64)
-        filter_rows(c, p4x, y4, 24, 8, 32, 96)
+        quarter_blocks_of_rows([(c, 6, 0), (c, 7, 4), (c, 16, 40), (c, 17, 44)])
+        half_blocks([(c, k) for k in (4, 5, 6, 7, 24, 25, 26, 27)])
+        quarter_blocks([(c, k) for k in (4, 5, 18, 19)])
+        filter_rows(c, px, y1, 48, 32, 128, 0, a1)
+        filter_rows(c, p2x, y2, 32, 16, 64, 64, a2)
+        filter_rows(c, p4x, y4, 24, 8, 32, 96, a4)
 
         @pl.when(has_e)
         def _():
@@ -447,12 +634,21 @@
         o2[...] = full_dot(value, w2[0], w2[1])
 
         def block(b, carry):
+            @pl.when((b == 1) & (c == CHUNKS - 1) & has_s)
+            def _():
+                end_row_copy.start()
+
+            @pl.when((b == 1) & (c == CHUNKS - 1) & has_w & has_s)
+            def _():
+                end_corner_copy.start()
+
             for part in range(2):
                 first = b * 16 + part * 8
                 start = pl.multiple_of(b * 32, 32)
                 sides = [halo(c, start, 32, part * 8 + r, 128) for r in range(8)]
                 rows = y1[c, pl.ds(first, 8)].reshape(256, 128)
-                value = full_dot(jnp.concatenate([rows, jnp.concatenate(sides, axis=0)], axis=1), w1[0], w1[1])
+                both = exact_dot(jnp.concatenate([rows, jnp.concatenate(sides, axis=0)], axis=1), w1[...])
+                value = both[:, :128] + both[:, 128:]
                 for r in range(8):
                     y = first + r
                     at2 = pl.multiple_of((b * 8 + part * 4 + r // 2) * 16, 16)
@@ -489,17 +685,9 @@
             packed = jnp.where(lane == y, roll(comb[y, pl.ds(h * 8, 8), :], y), packed)
         end_col_out[pl.ds(h * 8, 8), :] = packed
 
-    @pl.when(has_s)
-    def _():
-        end_row_copy.start()
-
     @pl.when(has_w)
     def _():
         end_col_copy.start()
-
-    @pl.when(has_w & has_s)
-    def _():
-        end_corner_copy.start()
 
     def send_waits(c, carry):
         @pl.when(has_n)
@@ -532,6 +720,7 @@
     @pl.when(has_n)
     def _():
         row_copy.wait_send()
+        dp_north.wait_send()
         end_row_copy.wait_recv()
 
     @pl.when(has_e & has_n)
@@ -546,6 +735,9 @@
     @pl.when(has_s)
     def _():
         end_row_copy.wait_send()
+        first_members.wait_send()
+        first_coarse.wait_send()
+        dp_south.wait_send()
 
     @pl.when(has_w)
     def _():
@@ -560,6 +752,7 @@
     lane = lax.broadcasted_iota(jnp.int32, (16, 128), 1)
     edge = jnp.where(lane == 32, roll(extra[2], 32), extra[1])
     half_edge = 0.5 * (edge + roll(edge, -1))
+    copies = []
     for block in range(4):
         rows = []
         for j in range(block * 8, block * 8 + 8):
@@ -576,20 +769,18 @@
                     flat[pl.ds(h * 8 * APAD + block * 16 + k, 8, stride=APAD), :] = value[
                         begin : begin + 8, side * 128 : side * 128 + 128
                     ]
-    copies = [
-        pltpu.make_async_copy(
-            ov.at[side, :, pl.ds(0, 64), :], out_hbm.at[:, :, pl.ds(side * 128, 128)], sem.at[side]
+    for side in range(2):
+        copy = pltpu.make_async_copy(
+            ov.at[side, :, pl.ds(0, 64), :], out_hbm.at[:, :, pl.ds(side * 128, 128)], sem.at[side, 0]
         )
-        for side in range(2)
-    ]
-    for copy in copies:
         copy.start()
+        copies.append(copy)
     for copy in copies:
         copy.wait()
 
 
 def shards(nx, ny, gradient, members):
-    filters, small, spread = constants()
+    filters, rows, small, spread = constants()
     w1, w2, w4 = (jnp.asarray(value) for value in filters)
     any_space = pl.BlockSpec(memory_space=pltpu.HBM)
     in_vmem = pl.BlockSpec(memory_space=pltpu.VMEM)
@@ -602,15 +793,16 @@
         functools.partial(main_kernel, nx, ny),
         name="localise",
         out_shape=(jax.ShapeDtypeStruct((32, 16, 128), F32), jax.ShapeDtypeStruct((3, 16, 128), F32)),
-        in_specs=[any_space] * 6,
+        in_specs=[any_space] * 7,
         out_specs=(in_vmem, in_vmem),
         scratch_shapes=[
-            vmem(2, LEV, 64, 128),
+            vmem(2, LEV, APAD, 128),
             vmem(MEM, LEV, MPAD, 128),
-            vmem(2, 256, 128, dtype=BF16),
+            vmem(256, 256, dtype=BF16),
             vmem(2, 256, 256, dtype=BF16),
             vmem(2, 256, 512, dtype=BF16),
-            vmem(2, 256, 128, dtype=BF16),
+            vmem(2, 3, 128, 512, dtype=BF16),
+            vmem(5, 256, 128, dtype=BF16),
             vmem(LEV, APAD, 128),
             vmem(32, 16, 128),
             vmem(CHUNKS, 48, 32, 128),
@@ -623,34 +815,47 @@
             vmem(2, CHUNKS, 112, 128),
             vmem(256, 256),
             vmem(64, 512),
-            vmem(8, 128),
-            vmem(8, 128),
+            vmem(16, 128),
+            vmem(16, 128),
             vmem(2, 16, 128),
             vmem(2, 16, 128),
             vmem(16, 128),
+            vmem(CHUNKS, 32, 128),
+            vmem(CHUNKS, 32, 128),
+            vmem(16, 128),
+            vmem(16, 128),
+            vmem(32, 128),
+            vmem(2, 32, 128),
+            vmem(CHUNKS, 32, 128),
+            vmem(CHUNKS, 32, 32, 128),
+            vmem(CHUNKS, 16, 16, 128),
+            vmem(CHUNKS, 8, 8, 128),
             vmem(16, 128),
             vmem(16, 128),
             vmem(16, 128),
             vmem(16, 128),
             dma((7,)),
+            dma((2, 3, CHUNKS)),
             dma((3,)),
             dma((3,)),
-            dma((2, CHUNKS, 4)),
-            dma((2, CHUNKS, 4)),
+            dma((4,)),
+            dma((4,)),
+            dma((2, CHUNKS, 3)),
+            dma((2, CHUNKS, 3)),
             dma((2, CHUNKS)),
             dma((2, CHUNKS)),
             dma((3,)),
             dma((3,)),
         ],
         compiler_params=pltpu.CompilerParams(collective_id=0, has_side_effects=True, vmem_limit_bytes=48 << 20),
-    )(*(pltpu.with_memory_space_constraint(value, pltpu.HBM) for value in (gradient, members, w1, w2, w4, jnp.asarray(small))))
+    )(*(pltpu.with_memory_space_constraint(value, pltpu.HBM) for value in (gradient, members, w1, w2, w4, jnp.asarray(rows), jnp.asarray(small))))
     return pl.pallas_call(
         spread_kernel,
         name="spread",
         out_shape=jax.ShapeDtypeStruct((LEV, 64, 256), F32),
         in_specs=[in_vmem] * 3,
         out_specs=any_space,
-        scratch_shapes=[vmem(2, LEV, APAD, 128), dma((2,))],
+        scratch_shapes=[vmem(2, LEV, APAD, 128), dma((2, 4))],
         compiler_params=pltpu.CompilerParams(vmem_limit_bytes=16 << 20),
     )(comb, extra, jnp.asarray(spread))
 

time: 35.8 us -> 33.5 us (0.936); the launches traced: 35.7 us -> 32.9 us
  Pallas kernels: 35.7 us -> 32.9 us
    pallas_call x1, Pallas kernels: 34.1 us -> 31.2 us  [shards(): pl.pallas_call(functools.partial(main_kernel, nx, ny), name='localise', o...]
where the time goes in v2:
time: 33.5 us; the launch traced here: 32.9 us
  Pallas kernels  32.9 us (98%)
    pallas_call x1, Pallas kernels, shards(): pl.pallas_call(functools.partial(main_kernel, nx, ny), name='localise', o...  31.2 us
    pallas_call x1, Pallas kernels, shards(): pl.pallas_call(spread_kernel, name='spread', out_shape=jax.ShapeDtypeStru...  1.7 us

profile of v2, /device:TPU:59, one launch (start us, length us, event | category | flops | bytes accessed | tf_op | source)
XLA Modules:
  0.0 32.9 jit_solution(16460606710722463685)
XLA Ops:
  0.0 0.0 copy-start
  0.0 31.2 %localise.1 = (f32[32,16,128]{2,1,0:T(8,128)S(1)}, f32[3,16,128]{2,1,0:T(8,128)S(1)}) custom-call(f32[16,64,256]{2,1,0:T(8,128)} %g_hbm.1, f32[8,16,32,128]{3,2,1,0:T(8,128)} %m_hbm.1, bf16[3,256,256]{2,1,0:T(8,128)(2,1)} %constant.12.clone.w1_hbm, bf16[3,2,256,256]{3,2,1,0:T(8,128)(2,1)} %constant.13.clone.w2_hbm, ...), custom_call_target="tpu_custom_call" | custom-call | tf_op jit(solution)/shard_map/localise/pallas_call | solution.py:792
  31.2 0.0 copy-done
  31.2 1.7 %spread.2 = f32[16,64,256]{2,1,0:T(8,128)} custom-call(f32[32,16,128]{2,1,0:T(8,128)S(1)} %get-tuple-element.7.comb, f32[3,16,128]{2,1,0:T(8,128)S(1)} %get-tuple-element.8.extra, bf16[256,256]{1,0:T(8,128)(2,1)S(1)} %copy-done), custom_call_target="tpu_custom_call" | custom-call | tf_op jit(solution)/shard_map/spread/pallas_call | solution.py:852
Async XLA Ops:
  0.0 31.2 %copy-start = (bf16[256,256]{1,0:T(8,128)(2,1)S(1)}, bf16[256,256]{1,0:T(8,128)(2,1)}, u32[]{:S(2)}) copy-start(bf16[256,256]{1,0:T(8,128)(2,1)} %constant.17.clone.spread) | copy-start | bytes 393220

commit v3 on v2

--- a/solution.py
+++ b/solution.py
@@ -13,7 +13,8 @@
 F32, BF16 = jnp.float32, jnp.bfloat16
 LEV, MEM = 16, 8
 CHUNKS = 4
-LAG = 2
+LAG = 3
+DEFER = 2
 MPAD = 40
 APAD = 72
 
@@ -137,11 +138,11 @@
 
 def main_kernel(
     nx, ny,
-    g_hbm, m_hbm, w1_hbm, w2_hbm, w4_hbm, wr_hbm, small_hbm,
-    comb, extra,
-    gv, mv, w1, w2, w4, wr, small,
+    g_hbm, m_hbm, w1_hbm, w2_hbm, w4_hbm, wr_hbm, small_hbm, spread_hbm,
+    out,
+    gv, mv, w1, w2, w4, wr, small, spread, comb,
     ac, cz, px, p2x, p4x, y1, y2, y4, sp, rp, o2, o4,
-    col_out, col_in, row_out, row_in, corner_in, m_out, m_in, c_out, c_in, dp, dp_in, add_rows, a1, a2, a4,
+    col_out, col_in, row_out, row_in, corner_in, m_out, m_in, c_out, c_in, c_next, dp, dp_in, add_rows, a1, a2, a4,
     end_row_in, end_col_out, end_col_in, end_corner_in,
     local_sem, wr_sem, s1, r1, sf, rf, ys, yr, xs, xr, s3, r3,
 ):
@@ -161,6 +162,7 @@
     w1_copy = pltpu.make_async_copy(w1_hbm.at[kind], w1, local_sem.at[3])
     w2_copy = pltpu.make_async_copy(w2_hbm.at[kind], w2, local_sem.at[4])
     w4_copy = pltpu.make_async_copy(w4_hbm.at[kind], w4, local_sem.at[5])
+    spread_copy = pltpu.make_async_copy(spread_hbm, spread, local_sem.at[7])
     row_kind = 1 - (gy == 0).astype(jnp.int32) + (gy == ny - 1).astype(jnp.int32)
     wr_copies = [
         pltpu.make_async_copy(
@@ -170,7 +172,7 @@
         )
         for part in range(2) for tile in range(3) for c in range(CHUNKS)
     ]
-    for copy in (g_copies[1], g_copies[0], small_copy, m_copy, *wr_copies, w1_copy, w2_copy, w4_copy):
+    for copy in (g_copies[1], g_copies[0], small_copy, m_copy, *wr_copies, w1_copy, w2_copy, w4_copy, spread_copy):
         copy.start()
 
     barrier = pltpu.get_barrier_semaphore()
@@ -240,19 +242,21 @@
     end_col_copy = remote(end_col_out, end_col_in, s3.at[1], r3.at[1], -1, 0)
     end_corner_copy = remote(comb.at[0], end_corner_in, s3.at[2], r3.at[2], -1, -1)
 
-    def y_copies(c, direction, pieces=slice(0, 3)):
+    def y_copies(c, direction, pieces=slice(0, 4)):
         if direction == 0:
             places = ((px, 32, 0, 8), (p2x, 16, 0, 4), (p4x, 8, 0, 4))
             dy = 1
         else:
             places = ((px, 9, 41, 7), (p2x, 12, 28, 4), (p4x, 12, 20, 4))
             dy = -1
+        ends = [(ref.at[c, pl.ds(src, n)], ref.at[c, pl.ds(dst, n)]) for ref, src, dst, n in places]
+        if direction == 1:
+            ends.append((m_out.at[c], m_in.at[c]))
         return [
-            remote(ref.at[c, pl.ds(src, n)], ref.at[c, pl.ds(dst, n)], ys.at[direction, c, i], yr.at[direction, c, i], 0, dy)
-            for i, (ref, src, dst, n) in list(enumerate(places))[pieces]
+            remote(src, dst, ys.at[direction, c, i], yr.at[direction, c, i], 0, dy)
+            for i, (src, dst) in list(enumerate(ends))[pieces]
         ]
 
-    first_members = remote(m_out, m_in, sf.at[0], rf.at[0], 0, -1)
     dp_north = remote(dp, dp_in.at[0], sf.at[2], rf.at[2], 0, 1)
     dp_south = remote(dp, dp_in.at[1], sf.at[3], rf.at[3], 0, -1)
     first_coarse = remote(c_out, c_in, sf.at[1], rf.at[1], 0, -1)
@@ -299,24 +303,6 @@
     for h in range(2):
         c_out[pl.ds(h * 8, 8), :] = across_row(0, h) + 0.5 * across_row(1, h)
 
-    pl.semaphore_wait(barrier, sum(there.astype(jnp.int32) for there, _, _ in around))
-
-    @pl.when(has_e)
-    def _():
-        col_copy.start()
-
-    @pl.when(has_n)
-    def _():
-        row_copy.start()
-
-    @pl.when(has_e & has_n)
-    def _():
-        corner_copy.start()
-
-    @pl.when(has_s)
-    def _():
-        first_coarse.start()
-
     def reduce_rows(j, carry):
         odd_rows = []
         for h in range(2):
@@ -332,6 +318,11 @@
         return mr[pl.ds(((2 * c + m2) * LEV + h * 8) * MPAD + y, 8, stride=MPAD), :]
 
     m_copy.wait()
+
+    for c in range(CHUNKS):
+        for m2 in range(2):
+            for h in range(2):
+                m_out[c, pl.ds(m2 * 16 + h * 8, 8), :] = member(c, m2, h, 0)
 
     def half_blocks(places):
         rows = []
@@ -378,7 +369,7 @@
             for copy in y_copies(c, 1, south):
                 copy.start()
 
-    everything, nothing = slice(0, 3), slice(0, 0)
+    everything, nothing = slice(0, 4), slice(0, 0)
 
     def later_rows(c):
         def row(y, carry):
@@ -416,10 +407,13 @@
         def _():
             dp_south.start()
 
-    def without_first_row(c, carry):
+    def own_rows(c):
         later_rows(c)
         half_blocks([(c, k) for k in range(12, 24)])
         quarter_blocks([(c, k) for k in range(12, 16)])
+
+    def without_first_row(c, carry):
+        own_rows(c)
         start_rows(c, slice(0, 2), everything)
         return carry
 
@@ -453,54 +447,69 @@
             cz[0, pl.ds(h * 8, 8), :] = c_out[pl.ds(h * 8, 8), :] + 0.5 * (before[h * 8 : h * 8 + 8] + corner)
 
     far = (gy % 8 == 0) & has_s
-    without_first_row(0, 0)
+    own_rows(0)
+    pl.semaphore_wait(barrier, sum(there.astype(jnp.int32) for there, _, _ in around))
+
+    @pl.when(has_e)
+    def _():
+        col_copy.start()
+
+    @pl.when(has_n)
+    def _():
+        row_copy.start()
+
+    @pl.when(has_e & has_n)
+    def _():
+        corner_copy.start()
 
     @pl.when(has_s)
     def _():
-        for c in range(CHUNKS):
-            for m2 in range(2):
-                for h in range(2):
-                    m_out[c, pl.ds(m2 * 16 + h * 8, 8), :] = member(c, m2, h, 0)
-        first_members.start()
+        first_coarse.start()
+
+    start_rows(0, slice(0, 2), everything)
 
     far_west = (gx % 4 == 0) & has_w
+    near_south = gy % 2 == 1
+    second = 1 + far_west.astype(jnp.int32)
 
     @pl.when(far_west)
     def _():
         without_first_row(1, 0)
 
+    @pl.when(near_south)
+    def _():
+        first_coarse_row()
+        first_row(0, 0)
+
     first_columns()
 
-    @pl.when(jnp.logical_not(far_west))
-    def _():
-        without_first_row(1, 0)
-
     @pl.when(far)
     def _():
-        lax.fori_loop(2, CHUNKS, without_first_row, 0)
-
-    first_coarse_row()
+        lax.fori_loop(second, CHUNKS, without_first_row, 0)
+
+    @pl.when(jnp.logical_not(near_south))
+    def _():
+        first_coarse_row()
+        first_row(0, 0)
 
     @pl.when(far)
     def _():
-        lax.fori_loop(0, CHUNKS, first_row, 0)
+        lax.fori_loop(1, CHUNKS, first_row, 0)
+
+    @pl.when(jnp.logical_not(far) & far_west)
+    def _():
+        first_row(1, 0)
 
     @pl.when(jnp.logical_not(far))
     def _():
-        lax.fori_loop(0, 2, first_row, 0)
-        lax.fori_loop(2, CHUNKS, whole, 0)
+        lax.fori_loop(second, CHUNKS, whole, 0)
 
     @pl.when(has_n)
     def _():
-        first_members.wait_recv()
         first_coarse.wait_recv()
         for h in range(2):
             corner = jnp.where(first_lane, 0.5 * roll(col_in[pl.ds(h * 8, 8), :], -63), 0.0)
-            coarse = c_in[pl.ds(h * 8, 8), :] + 0.5 * (across_row(63, h) + corner)
-            for c in range(CHUNKS):
-                for m2 in range(2):
-                    at_f = pl.ds(m2 * 16 + h * 8, 8)
-                    px[c, 40, at_f, :] = m_in[c, at_f, :] * coarse
+            c_next[pl.ds(h * 8, 8), :] = c_in[pl.ds(h * 8, 8), :] + 0.5 * (across_row(63, h) + corner)
 
     @pl.when(has_s)
     def _():
@@ -579,6 +588,10 @@
         for f in range(fields // 8):
             column(f, 0)
 
+    outer = (gy < 2) | (gy >= ny - 2)
+    defer_e = outer & has_e & (gx == nx // 2 - 1)
+    defer_w = outer & has_w & (gx == nx // 2)
+
     def rows_stage(c):
         spread_additions(c)
 
@@ -591,6 +604,13 @@
         def _():
             for copy in y_copies(c, 1):
                 copy.wait_recv()
+
+        @pl.when(has_n)
+        def _():
+            for m2 in range(2):
+                for h in range(2):
+                    at_f = pl.ds(m2 * 16 + h * 8, 8)
+                    px[c, 40, at_f, :] = m_in[c, at_f, :] * c_next[pl.ds(h * 8, 8), :]
 
         quarter_blocks_of_rows([(c, 6, 0), (c, 7, 4), (c, 16, 40), (c, 17, 44)])
         half_blocks([(c, k) for k in (4, 5, 6, 7, 24, 25, 26, 27)])
@@ -599,13 +619,23 @@
         filter_rows(c, p2x, y2, 32, 16, 64, 64, a2)
         filter_rows(c, p4x, y4, 24, 8, 32, 96, a4)
 
-        @pl.when(has_e)
+        @pl.when(has_e & (jnp.logical_not(defer_e) | (c > DEFER)))
         def _():
             x_copy(c, 0).start()
 
-        @pl.when(has_w)
+        @pl.when(has_w & (jnp.logical_not(defer_w) | (c > DEFER)))
         def _():
             x_copy(c, 1).start()
+
+        @pl.when(defer_e & (c == DEFER))
+        def _():
+            for chunk in range(DEFER + 1):
+                x_copy(chunk, 0).start()
+
+        @pl.when(defer_w & (c == DEFER))
+        def _():
+            for chunk in range(DEFER + 1):
+                x_copy(chunk, 1).start()
 
     comb[...] = jnp.zeros((32, 16, 128), F32)
     w1_copy.wait()
@@ -710,6 +740,26 @@
 
         return carry
 
+    spread_copy.wait()
+    flats = [out.at[side].reshape(LEV * APAD, 128) for side in range(2)]
+
+    def store_row(y, side, h, value):
+        flats[side][pl.ds(h * 8 * APAD + y, 8, stride=APAD), :] = value
+
+    def row_of(y, h):
+        return flats[1][pl.ds(h * 8 * APAD + y, 8, stride=APAD), :]
+
+    for block in range(4):
+        rows = []
+        for j in range(block * 8, block * 8 + 8):
+            rows += [comb[j], 0.5 * (comb[j] + comb[j + 1])] if j < 31 else [comb[j]]
+        value = exact_dot(jnp.concatenate(rows, axis=0), spread[pl.ds(0, 128), :])
+        for k in range(len(rows)):
+            for h in range(2):
+                for side in range(2):
+                    begin = k * 16 + h * 8
+                    store_row(block * 16 + k, side, h, value[begin : begin + 8, side * 128 : side * 128 + 128])
+
     lax.fori_loop(0, CHUNKS, send_waits, 0)
 
     @pl.when(has_e)
@@ -728,14 +778,21 @@
         corner_copy.wait_send()
         end_corner_copy.wait_recv()
 
-    extra[0] = end_row_in[...]
-    extra[1] = end_col_in[...]
-    extra[2] = end_corner_in[...]
+    for h in range(2):
+        levels = pl.ds(h * 8, 8)
+        edge = jnp.where(lane == 32, roll(end_corner_in[levels, :], 32), end_col_in[levels, :])
+        half_edge = 0.5 * (edge + roll(edge, -1))
+        for y in range(63):
+            add = roll((half_edge, edge)[y % 2 == 0], 127 - y // 2)
+            store_row(y, 1, h, row_of(y, h) + jnp.where(lane == 127, 0.5 * add, 0.0))
+        last = 0.5 * (comb[31, levels, :] + end_row_in[levels, :])
+        value = exact_dot(jnp.concatenate([last, roll(half_edge, -31)], axis=1), spread[...])
+        for side in range(2):
+            store_row(63, side, h, value[:, side * 128 : side * 128 + 128])
 
     @pl.when(has_s)
     def _():
         end_row_copy.wait_send()
-        first_members.wait_send()
         first_coarse.wait_send()
         dp_south.wait_send()
 
@@ -748,33 +805,15 @@
         end_corner_copy.wait_send()
 
 
-def spread_kernel(comb, extra, spread, out_hbm, ov, sem):
-    lane = lax.broadcasted_iota(jnp.int32, (16, 128), 1)
-    edge = jnp.where(lane == 32, roll(extra[2], 32), extra[1])
-    half_edge = 0.5 * (edge + roll(edge, -1))
-    copies = []
-    for block in range(4):
-        rows = []
-        for j in range(block * 8, block * 8 + 8):
-            here = comb[j]
-            later = comb[j + 1] if j < 31 else extra[0]
-            rows.append(jnp.concatenate([here, roll(edge, -j)], axis=1))
-            rows.append(jnp.concatenate([0.5 * (here + later), roll(half_edge, -j)], axis=1))
-        value = exact_dot(jnp.concatenate(rows, axis=0), spread[...])
-        for side in range(2):
-            flat = ov.at[side].reshape(LEV * APAD, 128)
-            for k in range(16):
-                for h in range(2):
-                    begin = k * 16 + h * 8
-                    flat[pl.ds(h * 8 * APAD + block * 16 + k, 8, stride=APAD), :] = value[
-                        begin : begin + 8, side * 128 : side * 128 + 128
-                    ]
-    for side in range(2):
-        copy = pltpu.make_async_copy(
-            ov.at[side, :, pl.ds(0, 64), :], out_hbm.at[:, :, pl.ds(side * 128, 128)], sem.at[side, 0]
+def output_kernel(padded, out_hbm, sem):
+    copies = [
+        pltpu.make_async_copy(
+            padded.at[side, :, pl.ds(0, 64), :], out_hbm.at[:, :, pl.ds(side * 128, 128)], sem.at[side]
         )
+        for side in range(2)
+    ]
+    for copy in copies:
         copy.start()
-        copies.append(copy)
     for copy in copies:
         copy.wait()
 
@@ -789,12 +828,12 @@
     def vmem(*shape, dtype=F32):
         return pltpu.VMEM(shape, dtype)
 
-    comb, extra = pl.pallas_call(
+    padded = pl.pallas_call(
         functools.partial(main_kernel, nx, ny),
         name="localise",
-        out_shape=(jax.ShapeDtypeStruct((32, 16, 128), F32), jax.ShapeDtypeStruct((3, 16, 128), F32)),
-        in_specs=[any_space] * 7,
-        out_specs=(in_vmem, in_vmem),
+        out_shape=jax.ShapeDtypeStruct((2, LEV, APAD, 128), F32),
+        in_specs=[any_space] * 8,
+        out_specs=in_vmem,
         scratch_shapes=[
             vmem(2, LEV, APAD, 128),
             vmem(MEM, LEV, MPAD, 128),
@@ -803,6 +842,8 @@
             vmem(2, 256, 512, dtype=BF16),
             vmem(2, 3, 128, 512, dtype=BF16),
             vmem(5, 256, 128, dtype=BF16),
+            vmem(256, 256, dtype=BF16),
+            vmem(32, 16, 128),
             vmem(LEV, APAD, 128),
             vmem(32, 16, 128),
             vmem(CHUNKS, 48, 32, 128),
@@ -824,6 +865,7 @@
             vmem(CHUNKS, 32, 128),
             vmem(16, 128),
             vmem(16, 128),
+            vmem(16, 128),
             vmem(32, 128),
             vmem(2, 32, 128),
             vmem(CHUNKS, 32, 128),
@@ -834,30 +876,30 @@
             vmem(16, 128),
             vmem(16, 128),
             vmem(16, 128),
-            dma((7,)),
+            dma((8,)),
             dma((2, 3, CHUNKS)),
             dma((3,)),
             dma((3,)),
             dma((4,)),
             dma((4,)),
-            dma((2, CHUNKS, 3)),
-            dma((2, CHUNKS, 3)),
+            dma((2, CHUNKS, 4)),
+            dma((2, CHUNKS, 4)),
             dma((2, CHUNKS)),
             dma((2, CHUNKS)),
             dma((3,)),
             dma((3,)),
         ],
         compiler_params=pltpu.CompilerParams(collective_id=0, has_side_effects=True, vmem_limit_bytes=48 << 20),
-    )(*(pltpu.with_memory_space_constraint(value, pltpu.HBM) for value in (gradient, members, w1, w2, w4, jnp.asarray(rows), jnp.asarray(small))))
+    )(*(pltpu.with_memory_space_constraint(value, pltpu.HBM) for value in (gradient, members, w1, w2, w4, jnp.asarray(rows), jnp.asarray(small), jnp.asarray(spread))))
     return pl.pallas_call(
-        spread_kernel,
-        name="spread",
+        output_kernel,
+        name="output",
         out_shape=jax.ShapeDtypeStruct((LEV, 64, 256), F32),
-        in_specs=[in_vmem] * 3,
+        in_specs=[in_vmem],
         out_specs=any_space,
-        scratch_shapes=[vmem(2, LEV, APAD, 128), dma((2, 4))],
-        compiler_params=pltpu.CompilerParams(vmem_limit_bytes=16 << 20),
-    )(comb, extra, jnp.asarray(spread))
+        scratch_shapes=[dma((2,))],
+        compiler_params=pltpu.CompilerParams(vmem_limit_bytes=8 << 20),
+    )(padded)
 
 
 def solution(mesh):

time: 33.5 us -> 31.5 us (0.940)
  Pallas kernels: 32.9 us -> 31.2 us
    pallas_call x1, Pallas kernels: 31.2 us -> 30.2 us  [shards(): pl.pallas_call(functools.partial(main_kernel, nx, ny), name='localise', o...]
    pallas_call x1, Pallas kernels: 1.7 us -> 0.99 us  [shards(): pl.pallas_call(output_kernel, name='output', out_shape=jax.ShapeDtypeStru...]
where the time goes in v3:
time: 31.5 us; the launch traced here: 31.2 us
  Pallas kernels  31.2 us (99%)
    pallas_call x1, Pallas kernels, shards(): pl.pallas_call(functools.partial(main_kernel, nx, ny), name='localise', o...  30.2 us
    pallas_call x1, Pallas kernels, shards(): pl.pallas_call(output_kernel, name='output', out_shape=jax.ShapeDtypeStru...  0.99 us

profile of v3, /device:TPU:59, one launch (start us, length us, event | category | flops | bytes accessed | tf_op | source)
XLA Modules:
  0.0 31.2 jit_solution(112468657659788592)
XLA Ops:
  0.0 30.2 %localise.1.padded = f32[2,16,72,128]{3,2,1,0:T(8,128)S(1)} custom-call(f32[16,64,256]{2,1,0:T(8,128)} %g_hbm.1, f32[8,16,32,128]{3,2,1,0:T(8,128)} %m_hbm.1, bf16[3,256,256]{2,1,0:T(8,128)(2,1)} %constant.12.clone.w1_hbm, bf16[3,2,256,256]{3,2,1,0:T(8,128)(2,1)} %constant.13.clone.w2_hbm, bf16[3,2,256,512]{3,2,1,0:T(8,128)(2,1)} %constant.14.clone.w4_hbm, ...), custom_call_target="tpu_custom_call" | custom-call | tf_op jit(solution)/shard_map/localise/pallas_call | solution.py:831
  30.2 1.0 %output.1 = f32[16,64,256]{2,1,0:T(8,128)} custom-call(f32[2,16,72,128]{3,2,1,0:T(8,128)S(1)} %localise.1.padded), custom_call_target="tpu_custom_call" | custom-call | tf_op jit(solution)/shard_map/output/pallas_call | solution.py:894

commit v4 on v3

--- a/solution.py
+++ b/solution.py
@@ -605,6 +605,16 @@
             for copy in y_copies(c, 1):
                 copy.wait_recv()
 
+        @pl.when(defer_e & (c == DEFER + 1))
+        def _():
+            for chunk in range(DEFER + 1):
+                x_copy(chunk, 0).start()
+
+        @pl.when(defer_w & (c == DEFER + 1))
+        def _():
+            for chunk in range(DEFER + 1):
+                x_copy(chunk, 1).start()
+
         @pl.when(has_n)
         def _():
             for m2 in range(2):
@@ -627,16 +637,6 @@
         def _():
             x_copy(c, 1).start()
 
-        @pl.when(defer_e & (c == DEFER))
-        def _():
-            for chunk in range(DEFER + 1):
-                x_copy(chunk, 0).start()
-
-        @pl.when(defer_w & (c == DEFER))
-        def _():
-            for chunk in range(DEFER + 1):
-                x_copy(chunk, 1).start()
-
     comb[...] = jnp.zeros((32, 16, 128), F32)
     w1_copy.wait()
     w2_copy.wait()
@@ -664,15 +664,16 @@
         o2[...] = full_dot(value, w2[0], w2[1])
 
         def block(b, carry):
-            @pl.when((b == 1) & (c == CHUNKS - 1) & has_s)
-            def _():
-                end_row_copy.start()
-
-            @pl.when((b == 1) & (c == CHUNKS - 1) & has_w & has_s)
-            def _():
-                end_corner_copy.start()
-
             for part in range(2):
+                if part == 1:
+                    @pl.when((b == 0) & (c == CHUNKS - 1) & has_s)
+                    def _():
+                        end_row_copy.start()
+
+                    @pl.when((b == 0) & (c == CHUNKS - 1) & has_w & has_s)
+                    def _():
+                        end_corner_copy.start()
+
                 first = b * 16 + part * 8
                 start = pl.multiple_of(b * 32, 32)
                 sides = [halo(c, start, 32, part * 8 + r, 128) for r in range(8)]

time: 31.5 us -> 32.6 us (1.035)
  the two profiles are of different devices: /device:TPU:59 before, /device:TPU:5 now
where the time goes in v4:
time: 32.6 us; the launch traced here: 32.5 us
  Pallas kernels  32.5 us (100%)
    pallas_call x1, Pallas kernels, shards(): pl.pallas_call(functools.partial(main_kernel, nx, ny), name='localise', o...  31.5 us
    pallas_call x1, Pallas kernels, shards(): pl.pallas_call(output_kernel, name='output', out_shape=jax.ShapeDtypeStru...  0.99 us

profile of v4, /device:TPU:5, one launch (start us, length us, event | category | flops | bytes accessed | tf_op | source)
XLA Modules:
  0.0 32.5 jit_solution(17565907589553486706)
XLA Ops:
  0.0 31.5 %localise.1.padded = f32[2,16,72,128]{3,2,1,0:T(8,128)S(1)} custom-call(f32[16,64,256]{2,1,0:T(8,128)} %g_hbm.1, f32[8,16,32,128]{3,2,1,0:T(8,128)} %m_hbm.1, bf16[3,256,256]{2,1,0:T(8,128)(2,1)} %constant.12.clone.w1_hbm, bf16[3,2,256,256]{3,2,1,0:T(8,128)(2,1)} %constant.13.clone.w2_hbm, bf16[3,2,256,512]{3,2,1,0:T(8,128)(2,1)} %constant.14.clone.w4_hbm, ...), custom_call_target="tpu_custom_call" | custom-call | tf_op jit(solution)/shard_map/localise/pallas_call | solution.py:832
  31.5 1.0 %output.1 = f32[16,64,256]{2,1,0:T(8,128)} custom-call(f32[2,16,72,128]{3,2,1,0:T(8,128)S(1)} %localise.1.padded), custom_call_target="tpu_custom_call" | custom-call | tf_op jit(solution)/shard_map/output/pallas_call | solution.py:895

commit v5 on v3

--- a/solution.py
+++ b/solution.py
@@ -14,7 +14,7 @@
 LEV, MEM = 16, 8
 CHUNKS = 4
 LAG = 3
-DEFER = 2
+DEFER = 3
 MPAD = 40
 APAD = 72
 

time: 31.5 us -> 31.1 us (0.987)
  the two profiles are of different devices: /device:TPU:59 before, /device:TPU:87 now
where the time goes in v5:
time: 31.1 us; the launch traced here: 31 us
  Pallas kernels  31 us (100%)
    pallas_call x1, Pallas kernels, shards(): pl.pallas_call(functools.partial(main_kernel, nx, ny), name='localise', o...  30 us
    pallas_call x1, Pallas kernels, shards(): pl.pallas_call(output_kernel, name='output', out_shape=jax.ShapeDtypeStru...  0.99 us

profile of v5, /device:TPU:87, one launch (start us, length us, event | category | flops | bytes accessed | tf_op | source)
XLA Modules:
  0.0 31.0 jit_solution(14189684110555933652)
XLA Ops:
  0.0 30.0 %localise.1.padded = f32[2,16,72,128]{3,2,1,0:T(8,128)S(1)} custom-call(f32[16,64,256]{2,1,0:T(8,128)} %g_hbm.1, f32[8,16,32,128]{3,2,1,0:T(8,128)} %m_hbm.1, bf16[3,256,256]{2,1,0:T(8,128)(2,1)} %constant.12.clone.w1_hbm, bf16[3,2,256,256]{3,2,1,0:T(8,128)(2,1)} %constant.13.clone.w2_hbm, bf16[3,2,256,512]{3,2,1,0:T(8,128)(2,1)} %constant.14.clone.w4_hbm, ...), custom_call_target="tpu_custom_call" | custom-call | tf_op jit(solution)/shard_map/localise/pallas_call | solution.py:831
  30.0 1.0 %output.1 = f32[16,64,256]{2,1,0:T(8,128)} custom-call(f32[2,16,72,128]{3,2,1,0:T(8,128)S(1)} %localise.1.padded), custom_call_target="tpu_custom_call" | custom-call | tf_op jit(solution)/shard_map/output/pallas_call | solution.py:894

commit v6 on v4

--- a/solution.py
+++ b/solution.py
@@ -664,16 +664,15 @@
         o2[...] = full_dot(value, w2[0], w2[1])
 
         def block(b, carry):
+            @pl.when((b == 1) & (c == CHUNKS - 1) & has_s)
+            def _():
+                end_row_copy.start()
+
+            @pl.when((b == 1) & (c == CHUNKS - 1) & has_w & has_s)
+            def _():
+                end_corner_copy.start()
+
             for part in range(2):
-                if part == 1:
-                    @pl.when((b == 0) & (c == CHUNKS - 1) & has_s)
-                    def _():
-                        end_row_copy.start()
-
-                    @pl.when((b == 0) & (c == CHUNKS - 1) & has_w & has_s)
-                    def _():
-                        end_corner_copy.start()
-
                 first = b * 16 + part * 8
                 start = pl.multiple_of(b * 32, 32)
                 sides = [halo(c, start, 32, part * 8 + r, 128) for r in range(8)]

time: 32.6 us -> 31.1 us (0.954)
  the two profiles are of different devices: /device:TPU:5 before, /device:TPU:59 now
where the time goes in v6:
time: 31.1 us; the launch traced here: 30.8 us
  Pallas kernels  30.8 us (99%)
    pallas_call x1, Pallas kernels, shards(): pl.pallas_call(functools.partial(main_kernel, nx, ny), name='localise', o...  29.8 us
    pallas_call x1, Pallas kernels, shards(): pl.pallas_call(output_kernel, name='output', out_shape=jax.ShapeDtypeStru...  0.99 us

profile of v6, /device:TPU:59, one launch (start us, length us, event | category | flops | bytes accessed | tf_op | source)
XLA Modules:
  0.0 30.8 jit_solution(17500919216821253286)
XLA Ops:
  0.0 29.8 %localise.1.padded = f32[2,16,72,128]{3,2,1,0:T(8,128)S(1)} custom-call(f32[16,64,256]{2,1,0:T(8,128)} %g_hbm.1, f32[8,16,32,128]{3,2,1,0:T(8,128)} %m_hbm.1, bf16[3,256,256]{2,1,0:T(8,128)(2,1)} %constant.12.clone.w1_hbm, bf16[3,2,256,256]{3,2,1,0:T(8,128)(2,1)} %constant.13.clone.w2_hbm, bf16[3,2,256,512]{3,2,1,0:T(8,128)(2,1)} %constant.14.clone.w4_hbm, ...), custom_call_target="tpu_custom_call" | custom-call | tf_op jit(solution)/shard_map/localise/pallas_call | solution.py:831
  29.8 1.0 %output.1 = f32[16,64,256]{2,1,0:T(8,128)} custom-call(f32[2,16,72,128]{3,2,1,0:T(8,128)S(1)} %localise.1.padded), custom_call_target="tpu_custom_call" | custom-call | tf_op jit(solution)/shard_map/output/pallas_call | solution.py:894
